TPU v7x, 128 devices: a whole 4x4x4 slice. The times are simulated.
128 devices in a mesh: replica: 1, heads: 16 (over z, y), model: 8 (over x, core).
Axes of the slice: x: 4, y: 4, z: 4, core: 2. Of those that a mesh axis runs over, the one named last changes fastest.
Arguments:
- tokens: bfloat16 [512, 8192], P('replica')
- w_query: bfloat16 [8192, 8192], P(None, ('heads', 'model'))
- w_key: bfloat16 [8192, 512], replicated
- w_value: bfloat16 [8192, 512], replicated
- w_out: bfloat16 [8192, 8192], P(('heads', 'model'))
- key_cache: bfloat16 [512, 8, 1024, 64], P(('replica', 'model'))
- value_cache: bfloat16 [512, 8, 1024, 64], P(('replica', 'model'))
- lengths: int32 [512], P(('replica', 'model'))
Outputs:
- output 1: bfloat16 [512, 8192], P('replica')
- output 2: bfloat16 [512, 8, 64], P(('replica', 'model'))
- output 3: bfloat16 [512, 8, 64], P(('replica', 'model'))
All inputs are finite; a program needn't handle non-finite values.
Results may differ from a plain program's by a relative error of at most 0.00223736.
Values are sent between devices in bfloat16 or wider.
A program may use at most 1 GiB of HBM per device.

v0:
```python
import jax
import jax.numpy as jnp
from jax import lax
from jax.sharding import PartitionSpec as P


def attend(queries, key_rows, value_rows, key_last, value_last, seq_len):
    score_scale = queries.shape[-1] ** -0.5
    scores = jnp.einsum("bgrd,bgtd->bgrt", queries, key_rows, preferred_element_type=jnp.float32) * score_scale
    score_new = jnp.einsum("bgrd,bgd->bgr", queries, key_last, preferred_element_type=jnp.float32) * score_scale
    positions = lax.broadcasted_iota(jnp.int32, (1, 1, 1, key_rows.shape[2]), 3)
    scores = jnp.where(positions < seq_len[:, None, None, None], scores, -jnp.inf)
    score_max = jnp.maximum(jnp.max(scores, axis=-1), score_new)
    weights = jnp.exp(scores - score_max[..., None])
    weight_new = jnp.exp(score_new - score_max)
    denom_sum = jnp.sum(weights, axis=-1) + weight_new
    weighted_sum = jnp.einsum("bgrt,bgtd->bgrd", weights.astype(jnp.bfloat16), value_rows, preferred_element_type=jnp.float32)
    weighted_sum = weighted_sum + weight_new.astype(jnp.bfloat16).astype(jnp.float32)[..., None] * value_last.astype(jnp.float32)[:, :, None, :]
    return (weighted_sum / denom_sum[..., None]).astype(jnp.bfloat16)


def solution(mesh):
    heads_count = mesh.shape["heads"]
    model_count = mesh.shape["model"]

    def local_step(tokens, w_query, w_key, w_value, w_out, key_cache, value_cache, lengths):
        batch_all = tokens.shape[0]
        local_rows = key_cache.shape[0]
        kv_count = key_cache.shape[1]
        head_dim = key_cache.shape[3]
        heads_local = w_query.shape[1] // head_dim
        heads_shard = heads_local * model_count
        group_size = heads_shard * heads_count // kv_count
        shard_groups = max(1, heads_shard // group_size)
        head_index = lax.axis_index("heads")
        model_index = lax.axis_index("model")
        queries = jnp.dot(tokens, w_query, preferred_element_type=jnp.float32).astype(jnp.bfloat16)
        queries = lax.all_to_all(queries.reshape(batch_all, heads_local, head_dim), "model", 0, 1, tiled=True)
        own_tokens = lax.dynamic_slice_in_dim(tokens, model_index * local_rows, local_rows, 0)
        key_new = jnp.dot(own_tokens, w_key, preferred_element_type=jnp.float32).astype(jnp.bfloat16)
        key_new = key_new.reshape(local_rows, kv_count, head_dim)
        value_new = jnp.dot(own_tokens, w_value, preferred_element_type=jnp.float32).astype(jnp.bfloat16)
        value_new = value_new.reshape(local_rows, kv_count, head_dim)
        first_group = head_index * heads_shard // group_size
        attended = attend(
            queries.reshape(local_rows, shard_groups, heads_shard // shard_groups, head_dim),
            lax.dynamic_slice_in_dim(key_cache, first_group, shard_groups, 1),
            lax.dynamic_slice_in_dim(value_cache, first_group, shard_groups, 1),
            lax.dynamic_slice_in_dim(key_new, first_group, shard_groups, 1),
            lax.dynamic_slice_in_dim(value_new, first_group, shard_groups, 1),
            lengths,
        )
        attended = lax.all_to_all(attended.reshape(local_rows, heads_shard, head_dim), "model", 1, 0, tiled=True)
        partial = jnp.dot(attended.reshape(batch_all, heads_local * head_dim), w_out, preferred_element_type=jnp.float32)
        mixed_sum = lax.psum(partial, ("heads", "model"))
        out_tokens = (tokens.astype(jnp.float32) + mixed_sum).astype(jnp.bfloat16)
        return (out_tokens, key_new, value_new)

    cache_spec = P(("replica", "model"), None, None, None)
    new_spec = P(("replica", "model"), None, None)
    return jax.shard_map(
        local_step,
        mesh=mesh,
        in_specs=(P("replica", None), P(None, ("heads", "model")), P(None, None), P(None, None), P(("heads", "model"), None), cache_spec, cache_spec, P(("replica", "model"))),
        out_specs=(P("replica", None), new_spec, new_spec),
        check_vma=False,
    )
```

profile of v0, /device:TPU:1, one launch (start us, length us, event | category | flops | bytes accessed | tf_op | source)
XLA Modules:
  0.0 297.5 jit_solution(14120727654267619219)
XLA Ops:
  7.2 0.0 copy-start
  7.2 0.0 copy-start.4
  7.2 6.4 %fusion.12 = bf16[512,1,64]{0,2,1:T(8,128)(2,1)S(1)} fusion(bf16[512,8192]{1,0:T(8,128)(2,1)} %param.8, bf16[8192,64]{0,1:T(8,128)(2,1)} %param.9), kind=kOutput, calls=%fused_computation.16 | convolution fusion | flops 536903680 | bytes 9502720 | tf_op jit(solution)/shard_map/dot_general | solution.py:37
  13.6 0.5 broadcast.30
  14.1 0.7 reduce.4
  14.7 0.1 copy.48
  14.9 0.8 reshape.116
  15.7 5.8 %all-to-all-start = ((bf16[8,2,2048]{2,1,0:T(2,128)(2,1)}), bf16[8,2,2048]{2,1,0:T(2,128)(2,1)S(1)}, u32[]{:S(2)}, u32[]{:S(2)}) async-start(bf16[8,2,2048]{2,1,0:T(2,128)(2,1)} %reshape.116), calls=%async_computation | async-start | bytes 131072 | tf_op jit(solution)/shard_map/all_to_all | solution.py:38
  21.5 0.0 all-reduce.2.cloned.1.call-start
  21.5 0.0 copy-done.4
  21.5 0.1 iota_compare_fusion
  21.6 5.3 %convolution_convert_fusion.1 = bf16[64,512]{1,0:T(8,128)(2,1)S(1)} fusion(bf16[8192,512]{1,0:T(8,128)(2,1)} %param.10, bf16[512,8192]{1,0:T(8,128)(2,1)} %param.8, s32[]{:T(128)S(6)} %select_n.22), kind=kOutput, calls=%fused_computation.14 | convolution fusion | flops 536903680 | bytes 9502724 | tf_op jit(solution)/shard_map/dot_general | solution.py:40
  26.9 5.3 %convolution_convert_fusion = bf16[64,512]{1,0:T(8,128)(2,1)S(1)} fusion(bf16[8192,512]{1,0:T(8,128)(2,1)} %param.11, bf16[512,8192]{1,0:T(8,128)(2,1)} %param.8, s32[]{:T(128)S(6)} %select_n.22), kind=kOutput, calls=%fused_computation.13 | convolution fusion | flops 536903680 | bytes 9502724 | tf_op jit(solution)/shard_map/dot_general | solution.py:42
  32.2 0.1 reshape.110
  32.3 0.0 copy-start.2
  32.3 0.1 reshape.107
  32.4 0.0 copy-start.3
  32.5 0.0 all-to-all-done
  32.6 0.1 reshape.117
  32.7 0.2 fusion.26
  32.9 4.7 %fusion.6 = (f32[64,8]{1,0:T(8,128)S(1)}, f32[64,8,1024]{2,1,0:T(8,128)S(1)}) fusion(pred[64,1024]{1,0:T(8,128)(4,1)S(1)} %iota_compare_fusion, bf16[64,8,1024,64]{2,3,1,0:T(8,128)(2,1)} %param.13, s32[]{:T(128)S(6)} %select_n.20, bf16[8,64,1,64]{3,1,0,2:T(8,128)(2,1)S(1)} %bitcast.49), kind=kOutput, calls=%fused_computation.9 | convolution fusion | flops 68681216 | bytes 10618884 | tf_op jit(solution)/shard_map/bgrd,bgtd->bgrt/dot_general | solution.py:9
  37.7 0.7 fusion.7
  38.4 5.8 %fusion.16 = bf16[64,8,64]{2,1,0:T(8,128)(2,1)S(1)} fusion(bf16[64,8,1024,64]{2,3,1,0:T(8,128)(2,1)} %param.14, s32[]{:T(128)S(6)} %select_n.20, f32[64,8,1024]{2,1,0:T(8,128)S(1)} %get-tuple-element.6, f32[64,8]{1,0:T(8,128)S(1)} %multiply_maximum_fusion, pred[64,1024]{1,0:T(8,128)(4,1)S(1)} %iota_compare_fusion, f32[64,8]{1,0:T(8,128)S(1)} %get-tuple-element.4, ...), kind=kOutput, calls=%fused_computation.18 | convolution fusion | flops 69337088 | bytes 10639364 | tf_op jit(solution)/shard_map/bgrt,bgtd->bgrd/dot_general | solution.py:17
  44.2 0.0 copy-done.2
  44.2 0.0 copy-done.3
  44.3 0.2 reshape.118
  44.4 9.5 %all_to_all.30 = bf16[8,2,2048]{2,1,0:T(2,128)(2,1)S(1)} all-to-all(bf16[8,2,2048]{2,1,0:T(2,128)(2,1)S(1)} %reshape.118), channel_id=1, replica_groups=mesh['replica'=1,'heads'=16,'model'=8] {'model'}, dimensions={0} | all-to-all | bytes 131072 | tf_op jit(solution)/shard_map/all_to_all | solution.py:53
  53.9 0.1 reshape.119
  54.0 0.0 copy-done
  54.0 8.0 %fusion.39 = f32[512,8192]{1,0:T(8,128)} fusion(bf16[512,64]{1,0:T(8,128)(2,1)S(1)} %bitcast.50, bf16[64,8192]{1,0:T(8,128)(2,1)S(1)} %copy-done), kind=kOutput, calls=%fused_computation.46 | convolution fusion | flops 536870912 | bytes 17891328 | tf_op jit(solution)/shard_map/dot_general | solution.py:54
  62.1 0.0 all-reduce.2.cloned.1.call-update
  62.1 216.3 %all-reduce.2.cloned.1.call-done = f32[512,8192]{1,0:T(8,128)} async-done(((f32[512,8192]{1,0:T(8,128)}), f32[512,8192]{1,0:T(8,128)}) %all-reduce.2.cloned.1.call-update) | async-done | bytes 16777232 | tf_op jit(solution)/shard_map/psum | solution.py:55
  278.4 0.0 copy-start.1
  278.4 12.2 %add_convert_fusion = bf16[512,8192]{1,0:T(8,128)(2,1)} fusion(f32[512,8192]{1,0:T(8,128)} %all-reduce.2.cloned.1.call-done, bf16[512,8192]{1,0:T(8,128)(2,1)} %param.8), kind=kLoop, calls=%fused_computation | loop fusion | flops 12582912 | bytes 33554432 | tf_op jit(solution)/shard_map/convert_element_type | solution.py:56
  290.7 0.0 copy-done.1
  (7 shorter events, 0.1 us)
Async XLA Ops:
  7.2 46.9 %copy-start = (bf16[64,8192]{1,0:T(8,128)(2,1)S(1)}, bf16[64,8192]{1,0:T(8,128)(2,1)}, u32[]{:S(2)}) copy-start(bf16[64,8192]{1,0:T(8,128)(2,1)} %param.12) | copy-start | bytes 3145732
  7.2 14.3 %copy-start.4 = (s32[64]{0:T(128)S(1)}, s32[64]{0:T(128)}, u32[]{:S(2)}) copy-start(s32[64]{0:T(128)} %param.15) | copy-start | bytes 772
  15.7 16.9 %all-to-all-start = ((bf16[8,2,2048]{2,1,0:T(2,128)(2,1)}), bf16[8,2,2048]{2,1,0:T(2,128)(2,1)S(1)}, u32[]{:S(2)}, u32[]{:S(2)}) async-start(bf16[8,2,2048]{2,1,0:T(2,128)(2,1)} %reshape.116), calls=%async_computation | async-start | bytes 131072 | tf_op jit(solution)/shard_map/all_to_all | solution.py:38
  21.5 257.0 %all-reduce.2.cloned.1.call-start = ((), (), s32[]{:S(2)}) async-start(), calls=%async_computation.2 | async-start | bytes 33554432 | tf_op jit(solution)/shard_map/psum | solution.py:55
  32.3 11.9 %copy-start.2 = (bf16[64,8,64]{2,1,0:T(8,128)(2,1)}, bf16[64,8,64]{2,1,0:T(8,128)(2,1)S(1)}, u32[]{:S(2)}) copy-start(bf16[64,8,64]{2,1,0:T(8,128)(2,1)S(1)} %reshape.110) | copy-start | bytes 196612
  32.4 11.8 %copy-start.3 = (bf16[64,8,64]{2,1,0:T(8,128)(2,1)}, bf16[64,8,64]{2,1,0:T(8,128)(2,1)S(1)}, u32[]{:S(2)}) copy-start(bf16[64,8,64]{2,1,0:T(8,128)(2,1)S(1)} %reshape.107) | copy-start | bytes 196612
  278.4 12.2 %copy-start.1 = (bf16[64,8192]{1,0:T(8,128)(2,1)S(1)}, bf16[64,8192]{1,0:T(8,128)(2,1)}, u32[]{:S(2)}) copy-start(bf16[64,8192]{1,0:T(8,128)(2,1)} %param.12) | copy-start | bytes 3145732
Sparse Core Ops, SparseCore 0:
  62.2 216.1 all-reduce.1
where the time goes:
time: 298 us; the launch traced here: 297 us
  waiting for transfers between devices  216 us (72%)
  matrix products  35.7 us (12%)
  between operations  14.2 us (5%)
  other arithmetic  13.7 us (5%)
  blocking collectives  9.45 us (3%)
  starting transfers between devices  5.8 us (2%)
    psum x1, waiting for transfers between devices, local_step(): mixed_sum = lax.psum(partial, ('heads', 'model'))  216 us
    convert_element_type x1, other arithmetic, local_step(): out_tokens = (tokens.astype(jnp.float32) + mixed_sum).astype(jnp.bfloat16)  12.2 us
    all_to_all x1, blocking collectives, local_step(): lax.all_to_all(attended.reshape(local_rows, heads_shard, head_dim), 'mode...  9.45 us
    dot_general x1, matrix products, local_step(): jnp.dot(attended.reshape(batch_all, heads_local * head_dim), w_out, prefe...  8.03 us
    dot_general x1, matrix products, local_step(): jnp.dot(tokens, w_query, preferred_element_type=jnp.float32)  6.36 us
  transfers between devices with their start and end apart: 2, of which 1 were waited for; matrix products, arithmetic and copies ran while one was open for 4% of the time, Pallas kernels for 0%

commit v1 on v0

--- a/solution.py
+++ b/solution.py
@@ -1,7 +1,320 @@
+import functools
+
 import jax
 import jax.numpy as jnp
 from jax import lax
+from jax.experimental import pallas as pl
+from jax.experimental.pallas import tpu as pltpu
 from jax.sharding import PartitionSpec as P
+
+MESH = pl.DeviceIdType.MESH
+RING = 4
+CHIPS = RING**3
+TILE_ROWS, LANES = 16, 128
+UNITS = 16
+COLOURS = ((0, 5), (5, 10), (10, 16))
+ORDERS = (("x", "y", "z"), ("y", "z", "x"), ("z", "x", "y"))
+STEPS = (1, 3, 2)
+SOURCES = (0, 3, 1, 2)
+
+
+class Place:
+    def __init__(self):
+        heads, model = lax.axis_index("heads"), lax.axis_index("model")
+        self.at = {"z": heads // RING, "y": heads % RING, "x": model // 2}
+        self.core = model % 2
+
+    def device(self, at, core):
+        return (0, at["z"] * RING + at["y"], at["x"] * 2 + core)
+
+    def along(self, axis, step):
+        at = dict(self.at)
+        at[axis] = (at[axis] + step) % RING
+        return self.device(at, self.core)
+
+    def sibling(self):
+        return self.device(self.at, 1 - self.core)
+
+    def chip(self):
+        return (self.at["z"] * RING + self.at["y"]) * RING + self.at["x"]
+
+    def offset(self, n):
+        at = {
+            "z": (self.at["z"] + n // (RING * RING)) % RING,
+            "y": (self.at["y"] + (n // RING) % RING) % RING,
+            "x": (self.at["x"] + n % RING) % RING,
+        }
+        return self.device(at, self.core), (at["z"] * RING + at["y"]) * RING + at["x"]
+
+
+def remote(src, dst, send_sem, recv_sem, device):
+    return pltpu.make_async_remote_copy(
+        src_ref=src, dst_ref=dst, send_sem=send_sem, recv_sem=recv_sem, device_id=device, device_id_type=MESH
+    )
+
+
+class Colour:
+    def __init__(self, place, held, order, recv, send, share=None):
+        self.place, self.held, self.recv, self.send, self.share = place, held, recv, send, share
+        self.axes = order
+        self.a, self.b, self.c = (place.at[axis] for axis in order)
+
+    def piece(self, row, n):
+        return self.held.at[self.c, (self.b + row) % RING, (self.a + n) % RING]
+
+    def row(self, plane, n):
+        return self.held.at[(self.c + plane) % RING, (self.b + n) % RING]
+
+    def copy(self, ref, phase, slot, n, step):
+        return remote(ref, ref, self.send.at[phase], self.recv.at[phase, slot, n], self.place.along(self.axes[phase], step))
+
+    def wait(self, ref, phase, slot, n):
+        self.copy(ref, phase, slot, n, 1).wait_recv()
+
+    def both(self, ref, phase, n):
+        self.copy(ref, phase, 0, n, 1).start()
+        self.copy(ref, phase, 1, n, 3).start()
+
+    def give(self, ref):
+        if self.share is not None:
+            remote(ref, ref, self.share.at[0], self.share.at[1], self.place.sibling()).start()
+
+    def open(self):
+        own = self.piece(0, 0)
+        for slot, step in enumerate(STEPS):
+            self.copy(own, 0, slot, 0, step).start()
+        self.both(own, 1, 0)
+
+    def line(self, t):
+        ref = self.piece(0, SOURCES[t])
+        self.wait(ref, 0, t - 1, 0)
+        self.both(ref, 1, t)
+
+    def own_row(self):
+        self.both(self.row(0, 0), 2, 0)
+        self.give(self.row(0, 0))
+
+    def near_pieces(self, t):
+        for slot, source, step in ((0, 3, 1), (1, 1, 3)):
+            ref = self.piece(source, SOURCES[t])
+            self.wait(ref, 1, slot, t)
+            if (t in (0, 3)) == (slot == 0):
+                self.copy(ref, 1, 2, t, step).start()
+
+    def near_rows(self):
+        for n in (1, 2):
+            ref = self.row(0, SOURCES[n])
+            self.both(ref, 2, n)
+            self.give(ref)
+
+    def far_row(self):
+        for t in range(RING):
+            self.wait(self.piece(2, SOURCES[t]), 1, 2, t)
+        self.both(self.row(0, 2), 2, 3)
+        self.give(self.row(0, 2))
+
+    def plane_rows(self, n):
+        for slot, source, step in ((0, 3, 1), (1, 1, 3)):
+            ref = self.row(source, SOURCES[n])
+            self.wait(ref, 2, slot, n)
+            if (n in (0, 3)) == (slot == 0):
+                self.copy(ref, 2, 2, n, step).start()
+            self.give(ref)
+
+    def far_plane_row(self, n):
+        ref = self.row(2, SOURCES[n])
+        self.wait(ref, 2, 2, n)
+        self.give(ref)
+
+    def close(self):
+        for ref, phase in ((self.held.at[0, 0, 0:3], 0), (self.held.at[0, 0:3], 1), (self.held.at[0:3], 2)):
+            remote(ref, ref, self.send.at[phase], self.recv.at[phase, 0, 0], self.place.sibling()).wait_send()
+
+    def close_share(self, other):
+        remote(self.held, other, self.share.at[0], self.share.at[1], self.place.sibling()).wait()
+
+
+def gather(colours):
+    for colour in colours:
+        colour.open()
+    for t in range(1, RING):
+        for colour in colours:
+            colour.line(t)
+    for colour in colours:
+        colour.own_row()
+    for t in range(RING):
+        for colour in colours:
+            colour.near_pieces(t)
+    for colour in colours:
+        colour.near_rows()
+    for colour in colours:
+        colour.plane_rows(0)
+    for colour in colours:
+        colour.far_row()
+    for n in range(1, RING):
+        for colour in colours:
+            colour.plane_rows(n)
+    for n in range(RING):
+        for colour in colours:
+            colour.far_plane_row(n)
+
+
+def project_kernel(
+    attended, w_out, tokens, *refs
+):
+    outs, (heads, w_all, residual, total, recv_in, send_in, recv_out, send_out, share, w_sems, local_sems) = refs[:3], (
+        refs[3:6],
+        *refs[6:],
+    )
+    place = Place()
+    chip, core = place.chip(), place.core
+
+    barrier = pltpu.get_barrier_semaphore()
+
+    def greet(n, carry):
+        device, _ = place.offset(n)
+        pl.semaphore_signal(barrier, inc=1, device_id=device, device_id_type=MESH)
+        return carry
+
+    lax.fori_loop(1, CHIPS, greet, 0)
+    pl.semaphore_signal(barrier, inc=1, device_id=place.sibling(), device_id_type=MESH)
+
+    def own_residual(n):
+        rows = pl.ds(pl.multiple_of(n * 128 + core * 64, 64), 64)
+        columns = pl.ds(pl.multiple_of(chip * LANES, LANES), LANES)
+        return pltpu.make_async_copy(tokens.at[rows, columns], residual.at[pl.ds(n * 64, 64)], local_sems.at[n])
+
+    for n in range(RING):
+        own_residual(n).start()
+
+    colours = [
+        Colour(place, heads[k], ORDERS[k], recv_in.at[k], send_in.at[k]) for k in range(3)
+    ]
+    for k, (first, last) in enumerate(COLOURS):
+        colour = colours[k]
+        for u in range(first, last):
+            i, j = u // 4, u % 4
+            heads[k][colour.c, colour.b, colour.a, u - first] = attended[
+                i * TILE_ROWS : (i + 1) * TILE_ROWS, j * LANES : (j + 1) * LANES
+            ]
+    own_columns = pl.ds(pl.multiple_of(chip * LANES, LANES), LANES)
+    w_all[chip, core] = w_out[:, own_columns]
+
+    pl.semaphore_wait(barrier, CHIPS)
+
+    def send_w(n, carry):
+        device, target = place.offset(n)
+        columns = pl.ds(pl.multiple_of(target * LANES, LANES), LANES)
+        remote(w_out.at[:, columns], w_all.at[chip, core], w_sems.at[0], w_sems.at[1], device).start()
+        return carry
+
+    lax.fori_loop(1, CHIPS, send_w, 0)
+    gather(colours)
+
+    w_arrived = w_all.at[pl.ds(0, CHIPS - 1), core]
+    remote(w_arrived, w_arrived, w_sems.at[0], w_sems.at[1], place.sibling()).wait()
+    w_mine, w_theirs = w_all.at[:, core], w_all.at[:, 1 - core]
+    remote(w_mine, w_mine, w_sems.at[2], w_sems.at[3], place.sibling()).start()
+    remote(w_mine, w_theirs, w_sems.at[2], w_sems.at[3], place.sibling()).wait()
+
+    for n in range(RING):
+        own_residual(n).wait()
+    total[...] = residual[...].astype(jnp.float32)
+
+    def tile(z, y, x, u):
+        k = next(k for k, (first, last) in enumerate(COLOURS) if first <= u < last)
+        at = {"z": z, "y": y, "x": x}
+        a, b, c = (at[axis] for axis in ORDERS[k])
+        return heads[k][c, b, a, u - COLOURS[k][0]]
+
+    def head_step(h, carry):
+        z, y = h // RING, h % RING
+        rows = [
+            jnp.concatenate([tile(z, y, x, i * 4 + j) for j in range(4)], axis=1) for x in range(RING) for i in range(4)
+        ]
+        lhs = jnp.concatenate(rows, axis=0)
+        rhs = w_all[pl.ds(h * RING, RING)].reshape(4 * LANES, LANES)
+        total[...] += jnp.dot(lhs, rhs, preferred_element_type=jnp.float32)
+        return carry
+
+    lax.fori_loop(0, RING * RING, head_step, 0)
+
+    out_colours = [
+        Colour(place, outs[k].at[core], ORDERS[k], recv_out.at[k], send_out.at[k], share.at[k]) for k in range(3)
+    ]
+    for k, (first, last) in enumerate(COLOURS):
+        colour = out_colours[k]
+        for u in range(first, last):
+            outs[k][core, colour.c, colour.b, colour.a, u - first] = total[
+                u * TILE_ROWS : (u + 1) * TILE_ROWS, :
+            ].astype(jnp.bfloat16)
+    for colour in colours:
+        colour.close()
+    gather(out_colours)
+    for k, colour in enumerate(out_colours):
+        colour.close()
+        colour.close_share(outs[k].at[1 - core])
+
+
+def project(attended, w_out, tokens):
+    held = [(RING, RING, RING, last - first, TILE_ROWS, LANES) for first, last in COLOURS]
+    vmem = pl.BlockSpec(memory_space=pltpu.VMEM)
+    return pl.pallas_call(
+        project_kernel,
+        out_shape=[jax.ShapeDtypeStruct((2, *shape), jnp.bfloat16) for shape in held],
+        in_specs=[vmem, vmem, pl.BlockSpec(memory_space=pl.ANY)],
+        out_specs=[vmem] * 3,
+        scratch_shapes=[pltpu.VMEM(shape, jnp.bfloat16) for shape in held]
+        + [
+            pltpu.VMEM((CHIPS, 2, 64, LANES), jnp.bfloat16),
+            pltpu.VMEM((256, LANES), jnp.bfloat16),
+            pltpu.VMEM((256, LANES), jnp.float32),
+            pltpu.SemaphoreType.DMA((3, 3, 3, 4)),
+            pltpu.SemaphoreType.DMA((3, 3)),
+            pltpu.SemaphoreType.DMA((3, 3, 3, 4)),
+            pltpu.SemaphoreType.DMA((3, 3)),
+            pltpu.SemaphoreType.DMA((3, 2)),
+            pltpu.SemaphoreType.DMA((4,)),
+            pltpu.SemaphoreType.DMA((4,)),
+        ],
+        compiler_params=pltpu.CompilerParams(collective_id=0, has_side_effects=True, vmem_limit_bytes=40 << 20),
+        name="project_and_gather",
+    )(attended, w_out, tokens)
+
+
+def lay_out_kernel(*refs):
+    held, (out, rows, sems) = refs[:3], refs[3:]
+    copies = []
+    for n in range(RING):
+        for core in range(2):
+            block = n * 2 + core
+            for i in range(4):
+                u = n * 4 + i
+                k = next(k for k, (first, last) in enumerate(COLOURS) if first <= u < last)
+                for chip in range(CHIPS):
+                    at = {"z": chip // 16, "y": chip // 4 % 4, "x": chip % 4}
+                    a, b, c = (at[axis] for axis in ORDERS[k])
+                    rows[block, i * TILE_ROWS : (i + 1) * TILE_ROWS, chip * LANES : (chip + 1) * LANES] = held[k][
+                        core, c, b, a, u - COLOURS[k][0]
+                    ]
+            copy = pltpu.make_async_copy(rows.at[block], out.at[pl.ds(block * 64, 64)], sems.at[block])
+            copy.start()
+            copies.append(copy)
+    for copy in copies:
+        copy.wait()
+
+
+def lay_out(held):
+    vmem = pl.BlockSpec(memory_space=pltpu.VMEM)
+    return pl.pallas_call(
+        lay_out_kernel,
+        out_shape=jax.ShapeDtypeStruct((512, CHIPS * LANES), jnp.bfloat16),
+        in_specs=[vmem] * 3,
+        out_specs=pl.BlockSpec(memory_space=pl.ANY),
+        scratch_shapes=[pltpu.VMEM((8, 64, CHIPS * LANES), jnp.bfloat16), pltpu.SemaphoreType.DMA((8,))],
+        compiler_params=pltpu.CompilerParams(vmem_limit_bytes=30 << 20),
+        name="lay_out",
+    )(*held)
 
 
 def attend(queries, key_rows, value_rows, key_last, value_last, seq_len):
@@ -50,11 +363,8 @@
             lax.dynamic_slice_in_dim(value_new, first_group, shard_groups, 1),
             lengths,
         )
-        attended = lax.all_to_all(attended.reshape(local_rows, heads_shard, head_dim), "model", 1, 0, tiled=True)
-        partial = jnp.dot(attended.reshape(batch_all, heads_local * head_dim), w_out, preferred_element_type=jnp.float32)
-        mixed_sum = lax.psum(partial, ("heads", "model"))
-        out_tokens = (tokens.astype(jnp.float32) + mixed_sum).astype(jnp.bfloat16)
-        return (out_tokens, key_new, value_new)
+        held = project(attended.reshape(local_rows, heads_shard * head_dim), w_out, tokens)
+        return (lay_out(held), key_new, value_new)
 
     cache_spec = P(("replica", "model"), None, None, None)
     new_spec = P(("replica", "model"), None, None)

time: 298 us -> 119 us (0.40)
  waiting for transfers between devices: 216 us -> 0.01 us
  Pallas kernels: 0 us -> 79.4 us
  between operations: 14.2 us -> 0.97 us
  other arithmetic: 13.7 us -> 1.5 us
  blocking collectives: 9.45 us -> 0 us
  matrix products: 35.7 us -> 27.3 us
    psum x1 -> x0, waiting for transfers between devices: 216 us -> none  [local_step(): mixed_sum = lax.psum(partial, ('heads', 'model'))]
    pallas_call x0 -> x2, Pallas kernels: none -> 79.4 us  [the longest x1 75.8 us: project(): pl.pallas_call(project_kernel, out_shape=[jax.ShapeDtypeStruct((2, *shape...]
    convert_element_type x1 -> x0, other arithmetic: 12.2 us -> none  [local_step(): out_tokens = (tokens.astype(jnp.float32) + mixed_sum).astype(jnp.bfloat16)]
    all_to_all x1 -> x0, blocking collectives: 9.45 us -> none  [local_step(): lax.all_to_all(attended.reshape(local_rows, heads_shard, head_dim), 'mode...]
    dot_general x1 -> x0, matrix products: 8.03 us -> none  [local_step(): jnp.dot(attended.reshape(batch_all, heads_local * head_dim), w_out, prefe...]
  transfers between devices with their start and end apart: 2 -> 1, of which waited for: 1 -> 0; matrix products, arithmetic and copies ran while one was open for 4% -> 9% of each run, Pallas kernels for 0% -> 0%
where the time goes in v1:
time: 119 us; the launch traced here: 118 us
  Pallas kernels  79.4 us (67%)
  matrix products  27.3 us (23%)
  starting transfers between devices  5.79 us (5%)
  local copies, waits for them, and re-layouts  3.29 us (3%)
  other arithmetic  1.5 us (1%)
    pallas_call x1, Pallas kernels, project(): pl.pallas_call(project_kernel, out_shape=[jax.ShapeDtypeStruct((2, *shape...  75.8 us
    dot_general x1, matrix products, local_step(): jnp.dot(tokens, w_query, preferred_element_type=jnp.float32)  6.04 us
    dot_general x1, matrix products, attend(): jnp.einsum('bgrt,bgtd->bgrd', weights.astype(jnp.bfloat16), value_rows, p...  5.84 us
    all_to_all x1, starting transfers between devices, local_step(): lax.all_to_all(queries.reshape(batch_all, heads_local, head_dim), 'model'...  5.79 us
    dot_general x1, matrix products, local_step(): jnp.dot(own_tokens, w_value, preferred_element_type=jnp.float32)  5.28 us
    dot_general x1, matrix products, local_step(): jnp.dot(own_tokens, w_key, preferred_element_type=jnp.float32)  5.28 us
    dot_general x1, matrix products, attend(): jnp.einsum('bgrd,bgtd->bgrt', queries, key_rows, preferred_element_type=j...  4.71 us
    pallas_call x1, Pallas kernels, lay_out(): pl.pallas_call(lay_out_kernel, out_shape=jax.ShapeDtypeStruct((512, CHIPS...  3.55 us
  transfers between devices with their start and end apart: 1, of which 0 were waited for; matrix products, arithmetic and copies ran while one was open for 9% of the time, Pallas kernels for 0%

profile of v1, /device:TPU:1, one launch (start us, length us, event | category | flops | bytes accessed | tf_op | source)
XLA Modules:
  0.0 118.3 jit_solution(17224502269327252715)
XLA Ops:
  0.6 0.0 copy-start
  0.6 0.0 copy-start.4
  0.7 1.2 %copy-done = bf16[8192,64]{0,1:T(8,128)(2,1)S(1)} copy-done((bf16[8192,64]{0,1:T(8,128)(2,1)S(1)}, bf16[8192,64]{0,1:T(8,128)(2,1)}, u32[]{:S(2)}) %copy-start) | copy-done | bytes 1048600
  1.9 6.0 %fusion.12 = bf16[512,1,64]{0,2,1:T(8,128)(2,1)S(1)} fusion(bf16[512,8192]{1,0:T(8,128)(2,1)} %tokens.1, bf16[8192,64]{0,1:T(8,128)(2,1)S(1)} %copy-done), kind=kOutput, calls=%fused_computation.15 | convolution fusion | flops 536903680 | bytes 9502720 | tf_op jit(solution)/shard_map/dot_general | solution.py:350
  7.9 0.5 broadcast.30
  8.4 0.7 reduce.4
  9.1 0.1 copy.40
  9.2 0.8 reshape.114
  10.0 5.8 %all-to-all-start = ((bf16[8,2,2048]{2,1,0:T(2,128)(2,1)}), bf16[8,2,2048]{2,1,0:T(2,128)(2,1)S(1)}, u32[]{:S(2)}, u32[]{:S(2)}) async-start(bf16[8,2,2048]{2,1,0:T(2,128)(2,1)} %reshape.114), calls=%async_computation | async-start | bytes 131072 | tf_op jit(solution)/shard_map/all_to_all | solution.py:351
  15.8 0.0 copy-done.4
  15.8 0.1 iota_compare_fusion
  15.9 5.3 %convolution_convert_fusion.1 = bf16[64,512]{1,0:T(8,128)(2,1)S(1)} fusion(bf16[8192,512]{1,0:T(8,128)(2,1)} %param.10, bf16[512,8192]{1,0:T(8,128)(2,1)} %tokens.1, s32[]{:T(128)S(6)} %select_n.22), kind=kOutput, calls=%fused_computation.13 | convolution fusion | flops 536903680 | bytes 9502724 | tf_op jit(solution)/shard_map/dot_general | solution.py:353
  21.2 5.3 %convolution_convert_fusion = bf16[64,512]{1,0:T(8,128)(2,1)S(1)} fusion(bf16[8192,512]{1,0:T(8,128)(2,1)} %param.11, bf16[512,8192]{1,0:T(8,128)(2,1)} %tokens.1, s32[]{:T(128)S(6)} %select_n.22), kind=kOutput, calls=%fused_computation.12 | convolution fusion | flops 536903680 | bytes 9502724 | tf_op jit(solution)/shard_map/dot_general | solution.py:355
  26.5 0.1 reshape.108
  26.6 0.0 copy-start.2
  26.6 0.1 reshape.105
  26.8 0.0 copy-start.3
  26.9 0.0 all-to-all-done
  26.9 0.1 reshape.115
  27.1 0.2 fusion.26
  27.3 4.7 %fusion.6 = (f32[64,8]{1,0:T(8,128)S(1)}, f32[64,8,1024]{2,1,0:T(8,128)S(1)}) fusion(pred[64,1024]{1,0:T(8,128)(4,1)S(1)} %iota_compare_fusion, bf16[64,8,1024,64]{2,3,1,0:T(8,128)(2,1)} %param.13, s32[]{:T(128)S(6)} %select_n.20, bf16[8,64,1,64]{3,1,0,2:T(8,128)(2,1)S(1)} %bitcast.38), kind=kOutput, calls=%fused_computation.8 | convolution fusion | flops 68681216 | bytes 10618884 | tf_op jit(solution)/shard_map/bgrd,bgtd->bgrt/dot_general | solution.py:322
  32.0 0.0 copy-start.1
  32.0 0.7 fusion.7
  32.7 5.8 %fusion.16 = bf16[64,8,64]{2,1,0:T(8,128)(2,1)S(1)} fusion(bf16[64,8,1024,64]{2,3,1,0:T(8,128)(2,1)} %param.14, s32[]{:T(128)S(6)} %select_n.20, f32[64,8,1024]{2,1,0:T(8,128)S(1)} %get-tuple-element.12, f32[64,8]{1,0:T(8,128)S(1)} %multiply_maximum_fusion, pred[64,1024]{1,0:T(8,128)(4,1)S(1)} %iota_compare_fusion, f32[64,8]{1,0:T(8,128)S(1)} %get-tuple-element.10, ...), kind=kOutput, calls=%fused_computation.17 | convolution fusion | flops 69337088 | bytes 10639364 | tf_op jit(solution)/shard_map/bgrt,bgtd->bgrd/dot_general | solution.py:330
  38.6 0.0 copy-done.2
  38.6 0.0 copy-done.3
  38.6 0.1 reshape.109.attended
  38.7 0.0 copy-done.1
  38.7 75.8 %project_and_gather.1 = (bf16[2,4,4,4,5,16,128]{6,5,4,3,2,1,0:T(8,128)(2,1)S(1)}, bf16[2,4,4,4,5,16,128]{6,5,4,3,2,1,0:T(8,128)(2,1)S(1)}, bf16[2,4,4,4,6,16,128]{6,5,4,3,2,1,0:T(8,128)(2,1)S(1)}) custom-call(bf16[64,512]{1,0:T(8,128)(2,1)S(1)} %reshape.109.attended, bf16[64,8192]{1,0:T(8,128)(2,1)S(1)} %copy-done.1, bf16[512,8192]{1,0:T(8,128)(2,1)} %tokens.1), custom_call_target="tpu_custom_call" | custom-call | tf_op jit(solution)/shard_map/project_and_gather/pallas_call | solution.py:262
  114.6 3.5 %lay_out.1 = bf16[512,8192]{1,0:T(8,128)(2,1)} custom-call(bf16[2,4,4,4,5,16,128]{6,5,4,3,2,1,0:T(8,128)(2,1)S(1)} %get-tuple-element.6.refs_0_, bf16[2,4,4,4,5,16,128]{6,5,4,3,2,1,0:T(8,128)(2,1)S(1)} %get-tuple-element.7.refs_1_, bf16[2,4,4,4,6,16,128]{6,5,4,3,2,1,0:T(8,128)(2,1)S(1)} %get-tuple-element.8.refs_2_), custom_call_target="tpu_custom_call" | custom-call | tf_op jit(solution)/shard_map/lay_out/pallas_call | solution.py:309
  (6 shorter events, 0.1 us)
Async XLA Ops:
  0.6 1.2 %copy-start = (bf16[8192,64]{0,1:T(8,128)(2,1)S(1)}, bf16[8192,64]{0,1:T(8,128)(2,1)}, u32[]{:S(2)}) copy-start(bf16[8192,64]{0,1:T(8,128)(2,1)} %param.9) | copy-start | bytes 3145732
  0.6 15.2 %copy-start.4 = (s32[64]{0:T(128)S(1)}, s32[64]{0:T(128)}, u32[]{:S(2)}) copy-start(s32[64]{0:T(128)} %param.15) | copy-start | bytes 772
  10.0 16.9 %all-to-all-start = ((bf16[8,2,2048]{2,1,0:T(2,128)(2,1)}), bf16[8,2,2048]{2,1,0:T(2,128)(2,1)S(1)}, u32[]{:S(2)}, u32[]{:S(2)}) async-start(bf16[8,2,2048]{2,1,0:T(2,128)(2,1)} %reshape.114), calls=%async_computation | async-start | bytes 131072 | tf_op jit(solution)/shard_map/all_to_all | solution.py:351
  26.6 11.9 %copy-start.2 = (bf16[64,8,64]{2,1,0:T(8,128)(2,1)}, bf16[64,8,64]{2,1,0:T(8,128)(2,1)S(1)}, u32[]{:S(2)}) copy-start(bf16[64,8,64]{2,1,0:T(8,128)(2,1)S(1)} %reshape.108) | copy-start | bytes 196612
  26.8 11.8 %copy-start.3 = (bf16[64,8,64]{2,1,0:T(8,128)(2,1)}, bf16[64,8,64]{2,1,0:T(8,128)(2,1)S(1)}, u32[]{:S(2)}) copy-start(bf16[64,8,64]{2,1,0:T(8,128)(2,1)S(1)} %reshape.105) | copy-start | bytes 196612
  32.0 6.7 %copy-start.1 = (bf16[64,8192]{1,0:T(8,128)(2,1)S(1)}, bf16[64,8192]{1,0:T(8,128)(2,1)}, u32[]{:S(2)}) copy-start(bf16[64,8192]{1,0:T(8,128)(2,1)} %w_out.1) | copy-start | bytes 3145732

commit v2 on v1

--- a/solution.py
+++ b/solution.py
@@ -10,9 +10,10 @@
 MESH = pl.DeviceIdType.MESH
 RING = 4
 CHIPS = RING**3
+HEAD = 64
 TILE_ROWS, LANES = 16, 128
 UNITS = 16
-COLOURS = ((0, 5), (5, 10), (10, 16))
+COLOURS = ((0, 6), (6, 10), (10, 16))
 ORDERS = (("x", "y", "z"), ("y", "z", "x"), ("z", "x", "y"))
 STEPS = (1, 3, 2)
 SOURCES = (0, 3, 1, 2)
@@ -134,73 +135,124 @@
         remote(self.held, other, self.share.at[0], self.share.at[1], self.place.sibling()).wait()
 
 
-def gather(colours):
-    for colour in colours:
-        colour.open()
-    for t in range(1, RING):
+def gather(colours, fillers=()):
+    fillers = list(fillers)
+    steps = [(Colour.open,)]
+    steps += [(Colour.line, t) for t in range(1, RING)]
+    steps += [(Colour.own_row,)]
+    steps += [(Colour.near_pieces, t) for t in range(RING)]
+    steps += [(Colour.near_rows,), (Colour.plane_rows, 0), (Colour.far_row,)]
+    steps += [(Colour.plane_rows, n) for n in range(1, RING)]
+    steps += [(Colour.far_plane_row, n) for n in range(RING)]
+    for step, *args in steps:
         for colour in colours:
-            colour.line(t)
-    for colour in colours:
-        colour.own_row()
-    for t in range(RING):
-        for colour in colours:
-            colour.near_pieces(t)
-    for colour in colours:
-        colour.near_rows()
-    for colour in colours:
-        colour.plane_rows(0)
-    for colour in colours:
-        colour.far_row()
-    for n in range(1, RING):
-        for colour in colours:
-            colour.plane_rows(n)
-    for n in range(RING):
-        for colour in colours:
-            colour.far_plane_row(n)
-
-
-def project_kernel(
-    attended, w_out, tokens, *refs
+            step(colour, *args)
+        if fillers:
+            fillers.pop(0)()
+    for filler in fillers:
+        filler()
+
+
+def step_kernel(
+    tokens, w_query, w_key, w_value, w_out, key_cache, value_cache, lengths,
+    out_a, out_b, out_c, key_new, value_new,
+    head_a, head_b, head_c, w_all, tok, wq, w_kv, keys, values, query, by_head, by_seq,
+    attended, to_seq, to_head, kv_own, total, residual,
+    recv_in, send_in, recv_out, send_out, share, w_sems, q_sems, local_sems,
 ):
-    outs, (heads, w_all, residual, total, recv_in, send_in, recv_out, send_out, share, w_sems, local_sems) = refs[:3], (
-        refs[3:6],
-        *refs[6:],
-    )
+    outs, heads = (out_a, out_b, out_c), (head_a, head_b, head_c)
     place = Place()
     chip, core = place.chip(), place.core
-
+    head_at, model_at = lax.axis_index("heads"), lax.axis_index("model")
+    group, half = head_at // 2, head_at % 2
     barrier = pltpu.get_barrier_semaphore()
 
-    def greet(n, carry):
-        device, _ = place.offset(n)
+    def partner(n):
+        other_half, other_model = (half + n // 8) % 2, (model_at + n % 8) % 8
+        return (0, group * 2 + other_half, other_model), other_half, other_model
+
+    def signal(device):
         pl.semaphore_signal(barrier, inc=1, device_id=device, device_id_type=MESH)
+
+    def greet_chip(n, carry):
+        signal(place.offset(n)[0])
         return carry
 
-    lax.fori_loop(1, CHIPS, greet, 0)
-    pl.semaphore_signal(barrier, inc=1, device_id=place.sibling(), device_id_type=MESH)
-
-    def own_residual(n):
+    lax.fori_loop(1, CHIPS, greet_chip, 0)
+    for n in range(RING):
+        for other_half in range(2):
+            signal((0, group * 2 + other_half, n * 2 + 1 - core))
+
+    def token_copy(n):
+        return pltpu.make_async_copy(tokens.at[:, pl.ds(n * 1024, 1024)], tok.at[n], local_sems.at[n])
+
+    wq_copy = pltpu.make_async_copy(w_query, wq, local_sems.at[8])
+    wq_copy.start()
+    for n in range(8):
+        token_copy(n).start()
+
+    def kv_block(n):
+        return (group // 2 + n) % 4
+
+    def w_kv_copy(which, n):
+        columns = pl.ds(pl.multiple_of(kv_block(n) * LANES, LANES), LANES)
+        source = (w_key, w_value)[which]
+        return pltpu.make_async_copy(source.at[:, columns], w_kv.at[which, n], local_sems.at[9 + which * 4 + n])
+
+    for which in range(2):
+        w_kv_copy(which, 0).start()
+
+    def cache_copy(which, n):
+        source, held = ((key_cache, keys), (value_cache, values))[which]
+        return pltpu.make_async_copy(
+            source.at[pl.ds(half * 32 + n * 8, 8), group], held.at[pl.ds(n * 8, 8)], local_sems.at[17 + which * 4 + n]
+        )
+
+    for n in range(4):
+        for which in range(2):
+            cache_copy(which, n).start()
+
+    def residual_copy(n):
         rows = pl.ds(pl.multiple_of(n * 128 + core * 64, 64), 64)
         columns = pl.ds(pl.multiple_of(chip * LANES, LANES), LANES)
-        return pltpu.make_async_copy(tokens.at[rows, columns], residual.at[pl.ds(n * 64, 64)], local_sems.at[n])
+        return pltpu.make_async_copy(tokens.at[rows, columns], residual.at[pl.ds(n * 64, 64)], local_sems.at[25 + n])
 
     for n in range(RING):
-        own_residual(n).start()
-
-    colours = [
-        Colour(place, heads[k], ORDERS[k], recv_in.at[k], send_in.at[k]) for k in range(3)
-    ]
-    for k, (first, last) in enumerate(COLOURS):
-        colour = colours[k]
-        for u in range(first, last):
-            i, j = u // 4, u % 4
-            heads[k][colour.c, colour.b, colour.a, u - first] = attended[
-                i * TILE_ROWS : (i + 1) * TILE_ROWS, j * LANES : (j + 1) * LANES
-            ]
-    own_columns = pl.ds(pl.multiple_of(chip * LANES, LANES), LANES)
-    w_all[chip, core] = w_out[:, own_columns]
-
-    pl.semaphore_wait(barrier, CHIPS)
+        residual_copy(n).start()
+    own_w = pltpu.make_async_copy(
+        w_out.at[:, pl.ds(pl.multiple_of(chip * LANES, LANES), LANES)], w_all.at[chip, core], local_sems.at[29]
+    )
+    own_w.start()
+    for n in range(1, 4):
+        for which in range(2):
+            w_kv_copy(which, n).start()
+
+    wq_copy.wait()
+    token_copy(0).wait()
+    both_last = (((1,), (1,)), ((), ()))
+
+    def query_part(n):
+        return lax.dot_general(tok[n], wq[:, n * 1024 : (n + 1) * 1024], both_last, preferred_element_type=jnp.float32)
+
+    acc = query_part(0)
+    for n in range(1, 8):
+        token_copy(n).wait()
+        acc = acc + query_part(n)
+    query[:, 0:HEAD] = acc.astype(jnp.bfloat16)
+    query[:, HEAD:LANES] = jnp.zeros((512, HEAD), jnp.bfloat16)
+
+    pl.semaphore_wait(barrier, CHIPS - 1 + 2 * RING)
+    slot = half * 8 + model_at
+
+    def query_rows(other_half, other_model):
+        return query.at[pl.ds(pl.multiple_of(other_model * 64 + other_half * 32, 32), 32)]
+
+    def send_query(n, carry):
+        device, other_half, other_model = partner(n)
+        remote(query_rows(other_half, other_model), by_head.at[slot], q_sems.at[0], q_sems.at[1], device).start()
+        return carry
+
+    lax.fori_loop(1, 16, send_query, 0)
 
     def send_w(n, carry):
         device, target = place.offset(n)
@@ -209,16 +261,105 @@
         return carry
 
     lax.fori_loop(1, CHIPS, send_w, 0)
-    gather(colours)
-
-    w_arrived = w_all.at[pl.ds(0, CHIPS - 1), core]
-    remote(w_arrived, w_arrived, w_sems.at[0], w_sems.at[1], place.sibling()).wait()
+    by_head[slot] = query_rows(half, model_at)[...]
+
+    own_rows = pl.ds(pl.multiple_of(model_at * 64, 64), 64)
+
+    def new_block(which, n):
+        w_kv_copy(which, n).wait()
+        acc = jnp.dot(tok[0, own_rows], w_kv[which, n, 0:1024], preferred_element_type=jnp.float32)
+        for k in range(1, 8):
+            acc = acc + jnp.dot(
+                tok[k, own_rows], w_kv[which, n, k * 1024 : (k + 1) * 1024], preferred_element_type=jnp.float32
+            )
+        acc = acc.astype(jnp.bfloat16)
+        columns = pl.ds(pl.multiple_of(kv_block(n) * LANES, LANES), LANES)
+        (key_new, value_new)[which][:, columns] = acc
+        if n == 0:
+            wide = acc.astype(jnp.float32)
+            wide = jnp.where(group % 2 == 0, wide, pltpu.roll(wide, HEAD, 1))
+            lanes = lax.broadcasted_iota(jnp.int32, wide.shape, 1)
+            kv_own[which] = jnp.where(lanes < HEAD, wide, 0.0)
+
+    for which in range(2):
+        new_block(which, 0)
+
+    row = lax.broadcasted_iota(jnp.int32, (512, 512), 0)
+    column = lax.broadcasted_iota(jnp.int32, (512, 512), 1)
+    to_seq[...] = (column == (row % 16) * 32 + row // 16).astype(jnp.float32).astype(jnp.bfloat16)
+    pair_row = lax.broadcasted_iota(jnp.int32, (256, 512), 0)
+    pair_column = lax.broadcasted_iota(jnp.int32, (256, 512), 1)
+    for parity in range(2):
+        source = (pair_row % 32) * 16 + (pair_row // 32) * 2 + parity
+        to_head[parity] = (pair_column == source).astype(jnp.float32).astype(jnp.bfloat16)
+
+    arrived = by_head.at[pl.ds(0, 15)]
+    remote(arrived, arrived, q_sems.at[0], q_sems.at[1], place.sibling()).wait()
+    by_seq[...] = jnp.dot(
+        to_seq[...], by_head[...].reshape(512, LANES), preferred_element_type=jnp.float32
+    ).astype(jnp.bfloat16)
+
+    positions = lax.broadcasted_iota(jnp.int32, (16, 1024), 1)
+    scale = HEAD**-0.5
+
+    def attend(s):
+        q = by_seq[pl.ds(pl.multiple_of(s * 16, 16), 16), 0:HEAD]
+        scores = jnp.dot(q, keys[s], preferred_element_type=jnp.float32) * scale
+        scores = jnp.where(positions < lengths[half * 32 + s], scores, -jnp.inf)
+        key_last = kv_own[0, pl.ds(half * 32 + s, 1), 0:HEAD]
+        value_last = kv_own[1, pl.ds(half * 32 + s, 1), 0:HEAD]
+        score_new = jnp.sum(q.astype(jnp.float32) * key_last, axis=1, keepdims=True) * scale
+        score_max = jnp.maximum(jnp.max(scores, axis=1, keepdims=True), score_new)
+        weights = jnp.exp(scores - score_max)
+        weight_new = jnp.exp(score_new - score_max)
+        denom = jnp.sum(weights, axis=1, keepdims=True) + weight_new
+        mixed = lax.dot_general(
+            weights.astype(jnp.bfloat16), values[s], both_last, preferred_element_type=jnp.float32
+        )
+        mixed = mixed + weight_new.astype(jnp.bfloat16).astype(jnp.float32) * value_last
+        attended[pl.ds(pl.multiple_of(s * 16, 16), 16), 0:HEAD] = (mixed / denom).astype(jnp.bfloat16)
+
+    attended[:, HEAD:LANES] = jnp.zeros((512, HEAD), jnp.bfloat16)
+    for n in range(4):
+        for which in range(2):
+            cache_copy(which, n).wait()
+
+        def attend_some(i, carry, n=n):
+            for s in range(4):
+                attend(n * 8 + i * 4 + s)
+            return carry
+
+        lax.fori_loop(0, 2, attend_some, 0)
+
+    low = attended[...]
+    high = pltpu.roll(low.astype(jnp.float32), HEAD, 1).astype(jnp.bfloat16)
+    block = jnp.dot(to_head[0], low, preferred_element_type=jnp.float32)
+    block = block + jnp.dot(to_head[1], high, preferred_element_type=jnp.float32)
+    block = block.astype(jnp.bfloat16)
+
+    colours = [Colour(place, heads[k], ORDERS[k], recv_in.at[k], send_in.at[k]) for k in range(3)]
+    for k, (first, last) in enumerate(COLOURS):
+        colour = colours[k]
+        for u in range(first, last):
+            heads[k][colour.c, colour.b, colour.a, u - first] = block[u * TILE_ROWS : (u + 1) * TILE_ROWS]
+
     w_mine, w_theirs = w_all.at[:, core], w_all.at[:, 1 - core]
-    remote(w_mine, w_mine, w_sems.at[2], w_sems.at[3], place.sibling()).start()
+
+    def share_w():
+        w_arrived = w_all.at[pl.ds(0, CHIPS - 1), core]
+        remote(w_arrived, w_arrived, w_sems.at[0], w_sems.at[1], place.sibling()).wait()
+        own_w.wait()
+        remote(w_mine, w_mine, w_sems.at[2], w_sems.at[3], place.sibling()).start()
+
+    def nothing():
+        pass
+
+    fillers = [functools.partial(new_block, which, n) for n in range(1, 4) for which in range(2)]
+    gather(colours, [nothing] * 2 + fillers + [nothing] * 2 + [share_w])
     remote(w_mine, w_theirs, w_sems.at[2], w_sems.at[3], place.sibling()).wait()
 
     for n in range(RING):
-        own_residual(n).wait()
+        residual_copy(n).wait()
     total[...] = residual[...].astype(jnp.float32)
 
     def tile(z, y, x, u):
@@ -227,17 +368,19 @@
         a, b, c = (at[axis] for axis in ORDERS[k])
         return heads[k][c, b, a, u - COLOURS[k][0]]
 
-    def head_step(h, carry):
-        z, y = h // RING, h % RING
+    def group_step(g, carry):
         rows = [
-            jnp.concatenate([tile(z, y, x, i * 4 + j) for j in range(4)], axis=1) for x in range(RING) for i in range(4)
+            jnp.concatenate([tile(g // 2, g % 2 * 2 + y, x, j * 2 + i) for j in range(8)], axis=1)
+            for x in range(RING)
+            for y in range(2)
+            for i in range(2)
         ]
         lhs = jnp.concatenate(rows, axis=0)
-        rhs = w_all[pl.ds(h * RING, RING)].reshape(4 * LANES, LANES)
+        rhs = w_all[pl.ds(g * 8, 8)].reshape(8 * LANES, LANES)
         total[...] += jnp.dot(lhs, rhs, preferred_element_type=jnp.float32)
         return carry
 
-    lax.fori_loop(0, RING * RING, head_step, 0)
+    lax.fori_loop(0, 8, group_step, 0)
 
     out_colours = [
         Colour(place, outs[k].at[core], ORDERS[k], recv_out.at[k], send_out.at[k], share.at[k]) for k in range(3)
@@ -256,30 +399,44 @@
         colour.close_share(outs[k].at[1 - core])
 
 
-def project(attended, w_out, tokens):
+def whole_step(*args):
     held = [(RING, RING, RING, last - first, TILE_ROWS, LANES) for first, last in COLOURS]
-    vmem = pl.BlockSpec(memory_space=pltpu.VMEM)
+    vmem, hbm = pl.BlockSpec(memory_space=pltpu.VMEM), pl.BlockSpec(memory_space=pl.ANY)
     return pl.pallas_call(
-        project_kernel,
-        out_shape=[jax.ShapeDtypeStruct((2, *shape), jnp.bfloat16) for shape in held],
-        in_specs=[vmem, vmem, pl.BlockSpec(memory_space=pl.ANY)],
-        out_specs=[vmem] * 3,
+        step_kernel,
+        out_shape=[jax.ShapeDtypeStruct((2, *shape), jnp.bfloat16) for shape in held]
+        + [jax.ShapeDtypeStruct((64, 512), jnp.bfloat16)] * 2,
+        in_specs=[hbm] * 7 + [pl.BlockSpec(memory_space=pltpu.SMEM)],
+        out_specs=[vmem] * 5,
         scratch_shapes=[pltpu.VMEM(shape, jnp.bfloat16) for shape in held]
         + [
             pltpu.VMEM((CHIPS, 2, 64, LANES), jnp.bfloat16),
+            pltpu.VMEM((8, 512, 1024), jnp.bfloat16),
+            pltpu.VMEM((64, 8192), jnp.bfloat16),
+            pltpu.VMEM((2, 4, 8192, LANES), jnp.bfloat16),
+            pltpu.VMEM((32, HEAD, 1024), jnp.bfloat16),
+            pltpu.VMEM((32, HEAD, 1024), jnp.bfloat16),
+            pltpu.VMEM((512, LANES), jnp.bfloat16),
+            pltpu.VMEM((16, 32, LANES), jnp.bfloat16),
+            pltpu.VMEM((512, LANES), jnp.bfloat16),
+            pltpu.VMEM((512, LANES), jnp.bfloat16),
+            pltpu.VMEM((512, 512), jnp.bfloat16),
+            pltpu.VMEM((2, 256, 512), jnp.bfloat16),
+            pltpu.VMEM((2, 64, LANES), jnp.float32),
+            pltpu.VMEM((256, LANES), jnp.float32),
             pltpu.VMEM((256, LANES), jnp.bfloat16),
-            pltpu.VMEM((256, LANES), jnp.float32),
             pltpu.SemaphoreType.DMA((3, 3, 3, 4)),
             pltpu.SemaphoreType.DMA((3, 3)),
             pltpu.SemaphoreType.DMA((3, 3, 3, 4)),
             pltpu.SemaphoreType.DMA((3, 3)),
             pltpu.SemaphoreType.DMA((3, 2)),
             pltpu.SemaphoreType.DMA((4,)),
-            pltpu.SemaphoreType.DMA((4,)),
+            pltpu.SemaphoreType.DMA((2,)),
+            pltpu.SemaphoreType.DMA((30,)),
         ],
-        compiler_params=pltpu.CompilerParams(collective_id=0, has_side_effects=True, vmem_limit_bytes=40 << 20),
-        name="project_and_gather",
-    )(attended, w_out, tokens)
+        compiler_params=pltpu.CompilerParams(collective_id=0, has_side_effects=True, vmem_limit_bytes=52 << 20),
+        name="whole_step",
+    )(*args)
 
 
 def lay_out_kernel(*refs):
@@ -317,54 +474,19 @@
     )(*held)
 
 
-def attend(queries, key_rows, value_rows, key_last, value_last, seq_len):
-    score_scale = queries.shape[-1] ** -0.5
-    scores = jnp.einsum("bgrd,bgtd->bgrt", queries, key_rows, preferred_element_type=jnp.float32) * score_scale
-    score_new = jnp.einsum("bgrd,bgd->bgr", queries, key_last, preferred_element_type=jnp.float32) * score_scale
-    positions = lax.broadcasted_iota(jnp.int32, (1, 1, 1, key_rows.shape[2]), 3)
-    scores = jnp.where(positions < seq_len[:, None, None, None], scores, -jnp.inf)
-    score_max = jnp.maximum(jnp.max(scores, axis=-1), score_new)
-    weights = jnp.exp(scores - score_max[..., None])
-    weight_new = jnp.exp(score_new - score_max)
-    denom_sum = jnp.sum(weights, axis=-1) + weight_new
-    weighted_sum = jnp.einsum("bgrt,bgtd->bgrd", weights.astype(jnp.bfloat16), value_rows, preferred_element_type=jnp.float32)
-    weighted_sum = weighted_sum + weight_new.astype(jnp.bfloat16).astype(jnp.float32)[..., None] * value_last.astype(jnp.float32)[:, :, None, :]
-    return (weighted_sum / denom_sum[..., None]).astype(jnp.bfloat16)
-
-
 def solution(mesh):
-    heads_count = mesh.shape["heads"]
-    model_count = mesh.shape["model"]
-
     def local_step(tokens, w_query, w_key, w_value, w_out, key_cache, value_cache, lengths):
-        batch_all = tokens.shape[0]
-        local_rows = key_cache.shape[0]
-        kv_count = key_cache.shape[1]
-        head_dim = key_cache.shape[3]
-        heads_local = w_query.shape[1] // head_dim
-        heads_shard = heads_local * model_count
-        group_size = heads_shard * heads_count // kv_count
-        shard_groups = max(1, heads_shard // group_size)
-        head_index = lax.axis_index("heads")
-        model_index = lax.axis_index("model")
-        queries = jnp.dot(tokens, w_query, preferred_element_type=jnp.float32).astype(jnp.bfloat16)
-        queries = lax.all_to_all(queries.reshape(batch_all, heads_local, head_dim), "model", 0, 1, tiled=True)
-        own_tokens = lax.dynamic_slice_in_dim(tokens, model_index * local_rows, local_rows, 0)
-        key_new = jnp.dot(own_tokens, w_key, preferred_element_type=jnp.float32).astype(jnp.bfloat16)
-        key_new = key_new.reshape(local_rows, kv_count, head_dim)
-        value_new = jnp.dot(own_tokens, w_value, preferred_element_type=jnp.float32).astype(jnp.bfloat16)
-        value_new = value_new.reshape(local_rows, kv_count, head_dim)
-        first_group = head_index * heads_shard // group_size
-        attended = attend(
-            queries.reshape(local_rows, shard_groups, heads_shard // shard_groups, head_dim),
-            lax.dynamic_slice_in_dim(key_cache, first_group, shard_groups, 1),
-            lax.dynamic_slice_in_dim(value_cache, first_group, shard_groups, 1),
-            lax.dynamic_slice_in_dim(key_new, first_group, shard_groups, 1),
-            lax.dynamic_slice_in_dim(value_new, first_group, shard_groups, 1),
+        *held, key_new, value_new = whole_step(
+            tokens,
+            w_query.T,
+            w_key,
+            w_value,
+            w_out,
+            jnp.swapaxes(key_cache, 2, 3),
+            jnp.swapaxes(value_cache, 2, 3),
             lengths,
         )
-        held = project(attended.reshape(local_rows, heads_shard * head_dim), w_out, tokens)
-        return (lay_out(held), key_new, value_new)
+        return (lay_out(held), key_new.reshape(64, 8, HEAD), value_new.reshape(64, 8, HEAD))
 
     cache_spec = P(("replica", "model"), None, None, None)
     new_spec = P(("replica", "model"), None, None)

time: 119 us -> 96.4 us (0.81)
  matrix products: 27.3 us -> 0 us
  Pallas kernels: 79.4 us -> 86.7 us
  starting transfers between devices: 5.79 us -> 0 us
  local copies, waits for them, and re-layouts: 3.29 us -> 8.81 us
  other arithmetic: 1.5 us -> 0 us
    dot_general x6 -> x0, matrix products: 27.3 us -> none  [the longest x1 6.04 us: local_step(): jnp.dot(tokens, w_query, preferred_element_type=jnp.float32)]
    pallas_call x1, Pallas kernels: 75.8 us -> 83.2 us  [whole_step(): pl.pallas_call(step_kernel, out_shape=[jax.ShapeDtypeStruct((2, *shape),...]
    all_to_all x1 -> x0, starting transfers between devices: 5.79 us -> none  [local_step(): lax.all_to_all(queries.reshape(batch_all, heads_local, head_dim), 'model'...]
    unnamed x15 -> x10, local copies, waits for them, and re-layouts: 2.33 us -> 7.23 us
  transfers between devices with their start and end apart: 1 -> 0, of which waited for: 0 -> 0; matrix products, arithmetic and copies ran while one was open for 9% -> 0% of each run, Pallas kernels for 0% -> 0%
where the time goes in v2:
time: 96.4 us; the launch traced here: 96.2 us
  Pallas kernels  86.7 us (90%)
  local copies, waits for them, and re-layouts  8.81 us (9%)
    pallas_call x1, Pallas kernels, whole_step(): pl.pallas_call(step_kernel, out_shape=[jax.ShapeDtypeStruct((2, *shape),...  83.2 us
    unnamed x10, local copies, waits for them, and re-layouts  7.23 us
    pallas_call x1, Pallas kernels, lay_out(): pl.pallas_call(lay_out_kernel, out_shape=jax.ShapeDtypeStruct((512, CHIPS...  3.55 us

profile of v2, /device:TPU:1, one launch (start us, length us, event | category | flops | bytes accessed | tf_op | source)
XLA Modules:
  0.0 96.2 jit_solution(8904418412548261323)
XLA Ops:
  0.6 0.0 copy-start.3
  0.6 1.2 %copy-done.3 = bf16[8192,64]{0,1:T(8,128)(2,1)S(1)} copy-done((bf16[8192,64]{0,1:T(8,128)(2,1)S(1)}, bf16[8192,64]{0,1:T(8,128)(2,1)}, u32[]{:S(2)}) %copy-start.3) | copy-done | bytes 1048600
  1.9 0.0 copy-start.4
  1.9 0.7 copy-done.4
  2.5 83.2 %whole_step.1 = (bf16[2,4,4,4,6,16,128]{6,5,4,3,2,1,0:T(8,128)(2,1)}, bf16[2,4,4,4,4,16,128]{6,5,4,3,2,1,0:T(8,128)(2,1)}, bf16[2,4,4,4,6,16,128]{6,5,4,3,2,1,0:...) custom-call(bf16[512,8192]{1,0:T(8,128)(2,1)} %tokens.1, bf16[64,8192]{1,0:T(8,128)(2,1)S(1)} %bitcast.3, ...), custom_call_target="tpu_custom_call" | custom-call | tf_op jit(solution)/shard_map/whole_step/pallas_call | solution.py:405
  85.7 0.0 copy-start
  85.7 1.9 %copy-done = bf16[2,4,4,4,6,16,128]{6,5,4,3,2,1,0:T(8,128)(2,1)S(1)} copy-done((bf16[2,4,4,4,6,16,128]{6,5,4,3,2,1,0:T(8,128)(2,1)S(1)}, bf16[2,4,4,4,6,16,128]{6,5,4,3,2,1,0:T(8,128)(2,1)}, u32[]{:S(2)}) %copy-start) | copy-done | bytes 3145752
  87.6 0.0 copy-start.1
  87.6 1.9 %copy-done.1 = bf16[2,4,4,4,6,16,128]{6,5,4,3,2,1,0:T(8,128)(2,1)S(1)} copy-done((bf16[2,4,4,4,6,16,128]{6,5,4,3,2,1,0:T(8,128)(2,1)S(1)}, bf16[2,4,4,4,6,16,128]{6,5,4,3,2,1,0:T(8,128)(2,1)}, u32[]{:S(2)}) %copy-start.1) | copy-done | bytes 3145752
  89.5 0.0 copy-start.2
  89.5 1.6 %copy-done.2 = bf16[2,4,4,4,4,16,128]{6,5,4,3,2,1,0:T(8,128)(2,1)S(1)} copy-done((bf16[2,4,4,4,4,16,128]{6,5,4,3,2,1,0:T(8,128)(2,1)S(1)}, bf16[2,4,4,4,4,16,128]{6,5,4,3,2,1,0:T(8,128)(2,1)}, u32[]{:S(2)}) %copy-start.2) | copy-done | bytes 2097176
  91.0 3.5 %lay_out.1 = bf16[512,8192]{1,0:T(8,128)(2,1)} custom-call(bf16[2,4,4,4,6,16,128]{6,5,4,3,2,1,0:T(8,128)(2,1)S(1)} %copy-done, bf16[2,4,4,4,4,16,128]{6,5,4,3,2,1,0:T(8,128)(2,1)S(1)} %copy-done.2, bf16[2,4,4,4,6,16,128]{6,5,4,3,2,1,0:T(8,128)(2,1)S(1)} %copy-done.1), custom_call_target="tpu_custom_call" | custom-call | tf_op jit(solution)/shard_map/lay_out/pallas_call | solution.py:466
  94.6 0.8 reshape.12
  95.4 0.8 reshape.13
Async XLA Ops:
  0.6 1.2 %copy-start.3 = (bf16[8192,64]{0,1:T(8,128)(2,1)S(1)}, bf16[8192,64]{0,1:T(8,128)(2,1)}, u32[]{:S(2)}) copy-start(bf16[8192,64]{0,1:T(8,128)(2,1)} %param.9) | copy-start | bytes 3145732
  1.9 0.7 copy-start.4
  85.7 1.9 %copy-start = (bf16[2,4,4,4,6,16,128]{6,5,4,3,2,1,0:T(8,128)(2,1)S(1)}, bf16[2,4,4,4,6,16,128]{6,5,4,3,2,1,0:T(8,128)(2,1)}, u32[]{:S(2)}) copy-start(bf16[2,4,4,4,6,16,128]{6,5,4,3,2,1,0:T(8,128)(2,1)} %get-tuple-element.8.refs_0_) | copy-start | bytes 9437188
  87.6 1.9 %copy-start.1 = (bf16[2,4,4,4,6,16,128]{6,5,4,3,2,1,0:T(8,128)(2,1)S(1)}, bf16[2,4,4,4,6,16,128]{6,5,4,3,2,1,0:T(8,128)(2,1)}, u32[]{:S(2)}) copy-start(bf16[2,4,4,4,6,16,128]{6,5,4,3,2,1,0:T(8,128)(2,1)} %get-tuple-element.10.refs_2_) | copy-start | bytes 9437188
  89.5 1.6 %copy-start.2 = (bf16[2,4,4,4,4,16,128]{6,5,4,3,2,1,0:T(8,128)(2,1)S(1)}, bf16[2,4,4,4,4,16,128]{6,5,4,3,2,1,0:T(8,128)(2,1)}, u32[]{:S(2)}) copy-start(bf16[2,4,4,4,4,16,128]{6,5,4,3,2,1,0:T(8,128)(2,1)} %get-tuple-element.9.refs_1_) | copy-start | bytes 6291460

commit v3 on v2

v3 whole, which is shorter than its diff:
```python
import functools

import jax
import jax.numpy as jnp
from jax import lax
from jax.experimental import pallas as pl
from jax.experimental.pallas import tpu as pltpu
from jax.sharding import PartitionSpec as P

MESH = pl.DeviceIdType.MESH
RING = 4
CHIPS = RING**3
HEAD = 64
TILE_ROWS, LANES = 16, 128
UNITS = 16
COLOURS = ((0, 5), (5, 10), (10, 16))
ORDERS = (("x", "y", "z"), ("y", "z", "x"), ("z", "x", "y"))
STEPS = (1, 3, 2)
SOURCES = (0, 3, 1, 2)


class Place:
    def __init__(self):
        heads, model = lax.axis_index("heads"), lax.axis_index("model")
        self.at = {"z": heads // RING, "y": heads % RING, "x": model // 2}
        self.core = model % 2
        self.ring = {axis: [(at + n) % RING for n in range(RING)] for axis, at in self.at.items()}

    def device(self, at, core):
        return (0, at["z"] * RING + at["y"], at["x"] * 2 + core)

    def along(self, axis, step):
        at = dict(self.at)
        at[axis] = self.ring[axis][step]
        return self.device(at, self.core)

    def sibling(self):
        return self.device(self.at, 1 - self.core)

    def chip(self):
        return (self.at["z"] * RING + self.at["y"]) * RING + self.at["x"]

    def others(self):
        for n in range(1, CHIPS):
            z, y, x = n // 16, n // 4 % 4, n % 4
            at = {"z": self.ring["z"][z], "y": self.ring["y"][y], "x": self.ring["x"][x]}
            yield self.device(at, self.core), (at["z"] * RING + at["y"]) * RING + at["x"]


def remote(src, dst, send_sem, recv_sem, device):
    return pltpu.make_async_remote_copy(
        src_ref=src, dst_ref=dst, send_sem=send_sem, recv_sem=recv_sem, device_id=device, device_id_type=MESH
    )


def order_of(k, core):
    return ORDERS[(k + core) % 3]


def by_core(core, first, second):
    return first + core * (second - first)


LINE, NEAR, FAR, PLANE, FAR_PLANE = (0, 16), (3, 32), (7, 16), (11, 32), (27, 64)
RECV_COUNT = 31


class Colour:
    def __init__(self, place, held, k, own, recv, send, share=None):
        self.held, self.own, self.recv, self.send, self.share = held, own, recv, send, share
        orders = [order_of(k, core) for core in range(2)]
        self.a, self.b, self.c = (by_core(place.core, place.at[p], place.at[q]) for p, q in zip(*orders))
        self.sibling = place.sibling()
        self.ring = []
        for p, q in zip(*orders):
            to = {}
            for step in STEPS:
                first, second = place.along(p, step), place.along(q, step)
                to[step] = tuple(by_core(place.core, i, j) for i, j in zip(first, second))
            self.ring.append(to)
        self.as_ = [(self.a + n) % RING for n in range(RING)]
        self.bs = [(self.b + n) % RING for n in range(RING)]
        self.cs = [(self.c + n) % RING for n in range(RING)]

    def piece(self, plane, row, t):
        return self.held.at[self.cs[plane], self.bs[row], self.as_[SOURCES[t]]]

    def row(self, plane, n):
        return self.held.at[self.cs[plane], self.bs[n]]

    def copy(self, ref, phase, kind, index, step, source=None):
        source = ref if source is None else source
        return remote(source, ref, self.send.at[phase], self.recv.at[kind[0] + index], self.ring[phase][step])

    def along_b(self, ref, t, source=None):
        self.copy(ref, 1, NEAR, t, 1, source).start()
        self.copy(ref, 1, NEAR, t, 3, source).start()

    def along_c(self, ref, n, t, source=None):
        self.copy(ref, 2, PLANE, n * 4 + t, 1, source).start()
        self.copy(ref, 2, PLANE, n * 4 + t, 3, source).start()

    def give(self, ref, source=None):
        if self.share is not None:
            source = ref if source is None else source
            remote(source, ref, self.share.at[0], self.share.at[1], self.sibling).start()

    def open(self):
        own = self.piece(0, 0, 0)
        for slot, step in enumerate(STEPS):
            self.copy(own, 0, LINE, slot, step, self.own).start()
        self.along_b(own, 0, self.own)
        self.along_c(own, 0, 0, self.own)
        self.give(own, self.own)

    def line(self, t):
        ref = self.piece(0, 0, t)
        self.along_b(ref, t)
        self.give(ref)

    def line_on(self, t):
        self.along_c(self.piece(0, 0, t), 0, t)

    def near(self, t):
        slot, row, step = (0, 3, 1) if t in (0, 3) else (1, 1, 3)
        self.copy(self.piece(0, row, t), 1, FAR, t, step).start()

    def near_on(self, t):
        for slot, row in enumerate((3, 1)):
            self.along_c(self.piece(0, row, t), 1 + slot, t)
            if t == 3:
                self.give(self.row(0, row))

    def far(self, t):
        self.along_c(self.piece(0, 2, t), 3, t)
        if t == 3:
            self.give(self.row(0, 2))

    def plane(self, n, t):
        plane, step = (3, 1) if t in (0, 3) else (1, 3)
        self.copy(self.piece(plane, SOURCES[n], t), 2, FAR_PLANE, n, step).start()
        if t == 3:
            for plane in (3, 1):
                self.give(self.row(plane, SOURCES[n]))

    def far_plane(self, n):
        self.give(self.row(2, SOURCES[n]))

    def close(self):
        for ref, phase in ((self.held.at[0, 0, 0:3], 0), (self.held.at[0, 0:3], 1), (self.held.at[0:3], 2)):
            remote(ref, ref, self.send.at[phase], self.recv.at[0], self.sibling).wait_send()

    def close_share(self, other):
        remote(self.held, other, self.share.at[0], self.share.at[1], self.sibling).wait()


GATHER = [("open",)]
GATHER += [("line", t) for t in range(1, RING)]
GATHER += [("line_on", t) for t in range(1, RING)]
for _t in range(RING):
    GATHER += [("near", _t), ("near_on", _t), ("plane", 0, _t)]
for _t in range(RING):
    GATHER += [("far", _t), ("plane", 1, _t), ("plane", 2, _t)]
GATHER += [("plane", 3, _t) for _t in range(RING)]
GATHER += [("far_plane", _n) for _n in range(RING)]


def gather(colours, tiles, fillers=None):
    fillers = fillers or {}
    first = colours[0]

    def wait(kind, index):
        ref = tiles(kind[1])
        remote(ref, ref, first.send.at[0], first.recv.at[kind[0] + index], first.sibling).wait_recv()

    for step in GATHER:
        if step[0] == "line":
            wait(LINE, step[1] - 1)
        elif step[0] == "near":
            wait(NEAR, step[1])
        elif step[0] == "far":
            wait(FAR, step[1])
        elif step[0] == "plane":
            wait(PLANE, step[1] * 4 + step[2])
        elif step[0] == "far_plane":
            wait(FAR_PLANE, step[1])
        for colour in colours:
            getattr(colour, step[0])(*step[1:])
        for filler in fillers.get(step, ()):
            filler()


def step_kernel(
    tokens, w_query, w_key, w_value, w_out_hbm, key_cache, value_cache, lengths_hbm,
    out_a, out_b, out_c, own_out, key_new, value_new,
    head_a, head_b, head_c, w_all, w_out, tok, wq, w_kv, keys, values, query, by_head, by_seq,
    attended, to_seq, to_head, kv_own, total, residual, lengths,
    recv_in, send_in, recv_out, send_out, share, w_sems, q_sems, local_sems,
):
    outs, heads = (out_a, out_b, out_c), (head_a, head_b, head_c)
    place = Place()
    chip, core = place.chip(), place.core
    head_at, model_at = lax.axis_index("heads"), lax.axis_index("model")
    group, half = head_at // 2, head_at % 2
    barrier = pltpu.get_barrier_semaphore()

    halves = [half, 1 - half]
    models = [(model_at + n) % 8 for n in range(8)]

    def partner(n):
        other_half, other_model = halves[n // 8], models[n % 8]
        return (0, group * 2 + other_half, other_model), other_half, other_model

    def signal(device):
        pl.semaphore_signal(barrier, inc=1, device_id=device, device_id_type=MESH)

    def greet():
        for device, _ in place.others():
            signal(device)
        for n in range(RING):
            for other_half in range(2):
                signal((0, group * 2 + other_half, n * 2 + 1 - core))

    def token_copy(n):
        return pltpu.make_async_copy(tokens.at[:, pl.ds(n * 1024, 1024)], tok.at[n], local_sems.at[n])

    wq_copy = pltpu.make_async_copy(w_query, wq, local_sems.at[8])
    wq_copy.start()
    for n in range(8):
        token_copy(n).start()

    def kv_block(n):
        return (group // 2 + n) % 4

    def w_kv_copy(which, n):
        columns = pl.ds(pl.multiple_of(kv_block(n) * LANES, LANES), LANES)
        source = (w_key, w_value)[which]
        return pltpu.make_async_copy(source.at[:, columns], w_kv.at[which, n % 2], local_sems.at[9 + which * 4 + n])

    own_w = pltpu.make_async_copy(w_out_hbm, w_out, local_sems.at[29])
    own_w.start()
    for which in range(2):
        w_kv_copy(which, 0).start()

    def cache_copy(which, n):
        source, held = ((key_cache, keys), (value_cache, values))[which]
        return pltpu.make_async_copy(
            source.at[pl.ds(half * 32 + n * 8, 8), group], held.at[pl.ds(n * 8, 8)], local_sems.at[17 + which * 4 + n]
        )

    for n in range(4):
        for which in range(2):
            cache_copy(which, n).start()

    def residual_copy(n):
        rows = pl.ds(pl.multiple_of(n * 128 + core * 64, 64), 64)
        columns = pl.ds(pl.multiple_of(chip * LANES, LANES), LANES)
        return pltpu.make_async_copy(tokens.at[rows, columns], residual.at[pl.ds(n * 64, 64)], local_sems.at[25 + n])

    for n in range(RING):
        residual_copy(n).start()
    for which in range(2):
        w_kv_copy(which, 1).start()

    lengths_copy = pltpu.make_async_copy(lengths_hbm, lengths, local_sems.at[30])
    lengths_copy.start()
    greet()

    wq_copy.wait()
    token_copy(0).wait()
    both_last = (((1,), (1,)), ((), ()))

    def query_part(n):
        part = wq[:, n * 1024 : (n + 1) * 1024]
        return [
            lax.dot_general(tok[n, r : r + 256], part, both_last, preferred_element_type=jnp.float32) for r in (0, 256)
        ]

    acc = query_part(0)
    for n in range(1, 8):
        token_copy(n).wait()
        acc = [a + p for a, p in zip(acc, query_part(n))]
    for i, a in enumerate(acc):
        query[i * 256 : (i + 1) * 256, 0:HEAD] = a.astype(jnp.bfloat16)
    query[:, HEAD:LANES] = jnp.zeros((512, HEAD), jnp.bfloat16)

    pl.semaphore_wait(barrier, CHIPS - 1 + 2 * RING)
    slot = half * 8 + model_at

    def query_rows(other_half, other_model):
        return query.at[pl.ds(pl.multiple_of(other_model * 64 + other_half * 32, 32), 32)]

    for n in range(1, 16):
        device, other_half, other_model = partner(n)
        remote(query_rows(other_half, other_model), by_head.at[slot], q_sems.at[0], q_sems.at[1], device).start()

    own_w.wait()
    for device, target in place.others():
        columns = pl.ds(pl.multiple_of(target * LANES, LANES), LANES)
        remote(w_out.at[:, columns], w_all.at[chip, core], w_sems.at[0], w_sems.at[1], device).start()
    w_all[chip, core] = w_out[:, pl.ds(pl.multiple_of(chip * LANES, LANES), LANES)]
    by_head[slot] = query_rows(half, model_at)[...]

    own_rows = pl.ds(pl.multiple_of(model_at * 64, 64), 64)

    def new_block(which, n):
        w_kv_copy(which, n).wait()
        acc = jnp.dot(tok[0, own_rows], w_kv[which, n % 2, 0:1024], preferred_element_type=jnp.float32)
        for k in range(1, 8):
            acc = acc + jnp.dot(
                tok[k, own_rows], w_kv[which, n % 2, k * 1024 : (k + 1) * 1024], preferred_element_type=jnp.float32
            )
        if n < 2:
            w_kv_copy(which, n + 2).start()
        acc = acc.astype(jnp.bfloat16)
        columns = pl.ds(pl.multiple_of(kv_block(n) * LANES, LANES), LANES)
        (key_new, value_new)[which][:, columns] = acc
        if n == 0:
            wide = acc.astype(jnp.float32)
            wide = jnp.where(group % 2 == 0, wide, pltpu.roll(wide, HEAD, 1))
            lanes = lax.broadcasted_iota(jnp.int32, wide.shape, 1)
            kv_own[which] = jnp.where(lanes < HEAD, wide, 0.0)

    for which in range(2):
        new_block(which, 0)

    row = lax.broadcasted_iota(jnp.int32, (512, 512), 0)
    column = lax.broadcasted_iota(jnp.int32, (512, 512), 1)
    to_seq[...] = (column == (row % 16) * 32 + row // 16).astype(jnp.float32).astype(jnp.bfloat16)
    pair_row = lax.broadcasted_iota(jnp.int32, (256, 512), 0)
    pair_column = lax.broadcasted_iota(jnp.int32, (256, 512), 1)
    for parity in range(2):
        source = (pair_row % 32) * 16 + (pair_row // 32) * 2 + parity
        to_head[parity] = (pair_column == source).astype(jnp.float32).astype(jnp.bfloat16)

    lengths_copy.wait()
    arrived = by_head.at[pl.ds(0, 15)]
    remote(arrived, arrived, q_sems.at[0], q_sems.at[1], place.sibling()).wait()
    by_seq[...] = jnp.dot(
        to_seq[...], by_head[...].reshape(512, LANES), preferred_element_type=jnp.float32
    ).astype(jnp.bfloat16)

    positions = lax.broadcasted_iota(jnp.int32, (16, 1024), 1)
    scale = HEAD**-0.5

    def attend(s):
        q = by_seq[pl.ds(pl.multiple_of(s * 16, 16), 16), 0:HEAD]
        scores = jnp.dot(q, keys[s], preferred_element_type=jnp.float32) * scale
        scores = jnp.where(positions < lengths[half * 32 + s], scores, -jnp.inf)
        key_last = kv_own[0, pl.ds(half * 32 + s, 1), 0:HEAD]
        value_last = kv_own[1, pl.ds(half * 32 + s, 1), 0:HEAD]
        score_new = jnp.sum(q.astype(jnp.float32) * key_last, axis=1, keepdims=True) * scale
        score_max = jnp.maximum(jnp.max(scores, axis=1, keepdims=True), score_new)
        weights = jnp.exp(scores - score_max)
        weight_new = jnp.exp(score_new - score_max)
        denom = jnp.sum(weights, axis=1, keepdims=True) + weight_new
        mixed = lax.dot_general(
            weights.astype(jnp.bfloat16), values[s], both_last, preferred_element_type=jnp.float32
        )
        mixed = mixed + weight_new.astype(jnp.bfloat16).astype(jnp.float32) * value_last
        attended[pl.ds(pl.multiple_of(s * 16, 16), 16), 0:HEAD] = (mixed / denom).astype(jnp.bfloat16)

    attended[:, HEAD:LANES] = jnp.zeros((512, HEAD), jnp.bfloat16)
    for n in range(4):
        for which in range(2):
            cache_copy(which, n).wait()

        def attend_some(i, carry, n=n):
            for s in range(4):
                attend(n * 8 + i * 4 + s)
            return carry

        lax.fori_loop(0, 2, attend_some, 0)

    low = attended[...]
    high = pltpu.roll(low.astype(jnp.float32), HEAD, 1).astype(jnp.bfloat16)
    block = jnp.dot(to_head[0], low, preferred_element_type=jnp.float32)
    block = block + jnp.dot(to_head[1], high, preferred_element_type=jnp.float32)
    block = block.astype(jnp.bfloat16)

    colours = [Colour(place, heads[k], k, None, recv_in, send_in.at[k]) for k in range(3)]
    for k, (first, last) in enumerate(COLOURS):
        colour = colours[k]
        for u in range(first, last):
            heads[k][colour.c, colour.b, colour.a, u - first] = block[u * TILE_ROWS : (u + 1) * TILE_ROWS]

    w_mine, w_theirs = w_all.at[:, core], w_all.at[:, 1 - core]

    def share_w():
        w_arrived = w_all.at[pl.ds(0, CHIPS - 1), core]
        remote(w_arrived, w_arrived, w_sems.at[0], w_sems.at[1], place.sibling()).wait()
        remote(w_mine, w_mine, w_sems.at[2], w_sems.at[3], place.sibling()).start()

    new_blocks = [functools.partial(new_block, which, n) for n in range(1, 4) for which in range(2)]
    def tiles(n):
        return tok.at[0, pl.ds(0, n * 2)]

    gather(colours, tiles, {("open",): new_blocks, ("plane", 2, 3): [share_w]})
    remote(w_mine, w_theirs, w_sems.at[2], w_sems.at[3], place.sibling()).wait()

    for n in range(RING):
        residual_copy(n).wait()
    total[...] = residual[...].astype(jnp.float32)

    def tile(z, y, x, u):
        k = next(k for k, (first, last) in enumerate(COLOURS) if first <= u < last)
        at = {"z": z, "y": y, "x": x}
        a, b, c = (by_core(core, at[p], at[q]) for p, q in zip(order_of(k, 0), order_of(k, 1)))
        return heads[k][c, b, a, u - COLOURS[k][0]]

    def group_step(g, carry):
        rows = [
            jnp.concatenate([tile(g // 2, g % 2 * 2 + y, x, j * 2 + i) for j in range(8)], axis=1)
            for x in range(RING)
            for y in range(2)
            for i in range(2)
        ]
        rhs = w_all[pl.ds(g * 8, 8)].reshape(8 * LANES, LANES)
        parts = [
            jnp.dot(jnp.concatenate(rows[n : n + 8], axis=0), rhs, preferred_element_type=jnp.float32) for n in (0, 8)
        ]
        for n, part in enumerate(parts):
            total[n * 128 : (n + 1) * 128] += part
        return carry

    lax.fori_loop(0, 8, group_step, 0)

    out_colours = [
        Colour(place, outs[k].at[core], k, own_out.at[first:last], recv_out, send_out.at[k], share.at[k])
        for k, (first, last) in enumerate(COLOURS)
    ]
    for u in range(UNITS):
        own_out[u] = total[u * TILE_ROWS : (u + 1) * TILE_ROWS, :].astype(jnp.bfloat16)
    for colour in colours:
        colour.close()
    gather(out_colours, tiles)
    for k, colour in enumerate(out_colours):
        colour.close()
        colour.close_share(outs[k].at[1 - core])


def whole_step(*args):
    held = [(RING, RING, RING, last - first, TILE_ROWS, LANES) for first, last in COLOURS]
    vmem, hbm = pl.BlockSpec(memory_space=pltpu.VMEM), pl.BlockSpec(memory_space=pltpu.HBM)
    return pl.pallas_call(
        step_kernel,
        out_shape=[pltpu.VMEM((2, *shape), jnp.bfloat16) for shape in held]
        + [jax.ShapeDtypeStruct((UNITS, TILE_ROWS, LANES), jnp.bfloat16)]
        + [jax.ShapeDtypeStruct((64, 512), jnp.bfloat16)] * 2,
        in_specs=[hbm] * 8,
        out_specs=[pl.BlockSpec(memory_space=pl.ANY)] * 3 + [vmem] * 3,
        scratch_shapes=[pltpu.VMEM(shape, jnp.bfloat16) for shape in held]
        + [
            pltpu.VMEM((CHIPS, 2, 64, LANES), jnp.bfloat16),
            pltpu.VMEM((64, 8192), jnp.bfloat16),
            pltpu.VMEM((8, 512, 1024), jnp.bfloat16),
            pltpu.VMEM((64, 8192), jnp.bfloat16),
            pltpu.VMEM((2, 2, 8192, LANES), jnp.bfloat16),
            pltpu.VMEM((32, HEAD, 1024), jnp.bfloat16),
            pltpu.VMEM((32, HEAD, 1024), jnp.bfloat16),
            pltpu.VMEM((512, LANES), jnp.bfloat16),
            pltpu.VMEM((16, 32, LANES), jnp.bfloat16),
            pltpu.VMEM((512, LANES), jnp.bfloat16),
            pltpu.VMEM((512, LANES), jnp.bfloat16),
            pltpu.VMEM((512, 512), jnp.bfloat16),
            pltpu.VMEM((2, 256, 512), jnp.bfloat16),
            pltpu.VMEM((2, 64, LANES), jnp.float32),
            pltpu.VMEM((256, LANES), jnp.float32),
            pltpu.VMEM((256, LANES), jnp.bfloat16),
            pltpu.SMEM((64,), jnp.int32),
            pltpu.SemaphoreType.DMA((RECV_COUNT,)),
            pltpu.SemaphoreType.DMA((3, 3)),
            pltpu.SemaphoreType.DMA((RECV_COUNT,)),
            pltpu.SemaphoreType.DMA((3, 3)),
            pltpu.SemaphoreType.DMA((3, 2)),
            pltpu.SemaphoreType.DMA((4,)),
            pltpu.SemaphoreType.DMA((2,)),
            pltpu.SemaphoreType.DMA((31,)),
        ],
        compiler_params=pltpu.CompilerParams(collective_id=0, has_side_effects=True, vmem_limit_bytes=42 << 20),
        name="whole_step",
    )(*args)


def lay_out_kernel(*refs):
    held, own, news, (out, key_out, value_out, rows, new_rows, sems) = refs[:3], refs[3], refs[4:6], refs[6:]
    place = Place()
    own_columns = pl.ds(pl.multiple_of(place.chip() * LANES, LANES), LANES)
    copies = []
    for n in range(RING):
        for core in range(2):
            block = n * 2 + core
            for i in range(4):
                u = n * 4 + i
                k = next(k for k, (first, last) in enumerate(COLOURS) if first <= u < last)
                for chip in range(CHIPS):
                    at = {"z": chip // 16, "y": chip // 4 % 4, "x": chip % 4}
                    a, b, c = (at[axis] for axis in order_of(k, core))
                    rows[block, i * TILE_ROWS : (i + 1) * TILE_ROWS, chip * LANES : (chip + 1) * LANES] = held[k][
                        core, c, b, a, u - COLOURS[k][0]
                    ]

            @pl.when(place.core == core)
            def _(n=n, block=block):
                for i in range(4):
                    rows[block, i * TILE_ROWS : (i + 1) * TILE_ROWS, own_columns] = own[n * 4 + i]

            copy = pltpu.make_async_copy(rows.at[block], out.at[pl.ds(block * 64, 64)], sems.at[block])
            copy.start()
            copies.append(copy)
    for which, target in enumerate((key_out, value_out)):
        wide = news[which][...].astype(jnp.float32)
        parts = [wide[:, g * HEAD : (g + 1) * HEAD] for g in range(8)]
        new_rows[which] = jnp.stack(parts, axis=1).astype(jnp.bfloat16)
        copy = pltpu.make_async_copy(new_rows.at[which], target, sems.at[8 + which])
        copy.start()
        copies.append(copy)
    for copy in copies:
        copy.wait()


def lay_out(*held):
    vmem = pl.BlockSpec(memory_space=pltpu.VMEM)
    return pl.pallas_call(
        lay_out_kernel,
        out_shape=[jax.ShapeDtypeStruct((512, CHIPS * LANES), jnp.bfloat16)]
        + [jax.ShapeDtypeStruct((64, 8, HEAD), jnp.bfloat16)] * 2,
        in_specs=[vmem] * 6,
        out_specs=[pl.BlockSpec(memory_space=pltpu.HBM)] * 3,
        scratch_shapes=[
            pltpu.VMEM((8, 64, CHIPS * LANES), jnp.bfloat16),
            pltpu.VMEM((2, 64, 8, HEAD), jnp.bfloat16),
            pltpu.SemaphoreType.DMA((10,)),
        ],
        compiler_params=pltpu.CompilerParams(vmem_limit_bytes=30 << 20),
        name="lay_out",
    )(*held)


def solution(mesh):
    def local_step(tokens, w_query, w_key, w_value, w_out, key_cache, value_cache, lengths):
        held = whole_step(
            tokens,
            pltpu.with_memory_space_constraint(w_query.T, pltpu.HBM),
            w_key,
            w_value,
            pltpu.with_memory_space_constraint(w_out, pltpu.HBM),
            jnp.swapaxes(key_cache, 2, 3),
            jnp.swapaxes(value_cache, 2, 3),
            pltpu.with_memory_space_constraint(lengths, pltpu.HBM),
        )
        return tuple(lay_out(*held))

    cache_spec = P(("replica", "model"), None, None, None)
    new_spec = P(("replica", "model"), None, None)
    return jax.shard_map(
        local_step,
        mesh=mesh,
        in_specs=(P("replica", None), P(None, ("heads", "model")), P(None, None), P(None, None), P(("heads", "model"), None), cache_spec, cache_spec, P(("replica", "model"))),
        out_specs=(P("replica", None), new_spec, new_spec),
        check_vma=False,
    )
```

time: 96.4 us -> 77.2 us (0.80)
  Pallas kernels: 86.7 us -> 76.4 us
  local copies, waits for them, and re-layouts: 8.81 us -> 0 us
    pallas_call x2, Pallas kernels: 86.7 us -> 76.4 us  [the longest x1 72.8 us: whole_step(): pl.pallas_call(step_kernel, out_shape=[pltpu.VMEM((2, *shape), jnp.bfloat...]
    unnamed x10 -> x0, local copies, waits for them, and re-layouts: 7.23 us -> none
    reshape x2 -> x0, local copies, waits for them, and re-layouts: 1.57 us -> none  [the longest x1 0.79 us: local_step(): key_new.reshape(64, 8, HEAD)]
where the time goes in v3:
time: 77.2 us; the launch traced here: 77.1 us
  Pallas kernels  76.4 us (99%)
    pallas_call x1, Pallas kernels, whole_step(): pl.pallas_call(step_kernel, out_shape=[pltpu.VMEM((2, *shape), jnp.bfloat...  72.8 us
    pallas_call x1, Pallas kernels, lay_out(): pl.pallas_call(lay_out_kernel, out_shape=[jax.ShapeDtypeStruct((512, CHIP...  3.61 us

profile of v3, /device:TPU:1, one launch (start us, length us, event | category | flops | bytes accessed | tf_op | source)
XLA Modules:
  0.0 77.1 jit_solution(18052009821269225523)
XLA Ops:
  0.6 72.8 %whole_step.1 = (bf16[2,4,4,4,5,16,128]{6,5,4,3,2,1,0:T(8,128)(2,1)S(1)}, bf16[2,4,4,4,5,16,128]{6,5,4,3,2,1,0:T(8,128)(2,1)S(1)}, bf16[2,4,4,4,6,16,128]{6,5,4,...) custom-call(bf16[512,8192]{1,0:T(8,128)(2,1)} %tokens.1, ...), custom_call_target="tpu_custom_call" | custom-call | tf_op jit(solution)/shard_map/whole_step/pallas_call | solution.py:445
  73.5 3.6 %lay_out.1 = (bf16[512,8192]{1,0:T(8,128)(2,1)}, bf16[64,8,64]{2,1,0:T(8,128)(2,1)}, bf16[64,8,64]{2,1,0:T(8,128)(2,1)}) custom-call(bf16[2,4,4,4,5,16,128]{6,5,4,3,2,1,0:T(8,128)(2,1)S(1)} %get-tuple-element.9.refs_0_, bf16[2,4,4,4,5,16,128]{6,5,4,3,2,1,0:T(8,128)(2,1)S(1)} %get-tuple-element.10.refs_1_, ...), custom_call_target="tpu_custom_call" | custom-call | tf_op jit(solution)/shard_map/lay_out/pallas_call | solution.py:524

commit v4 on v3

--- a/solution.py
+++ b/solution.py
@@ -10,6 +10,7 @@
 MESH = pl.DeviceIdType.MESH
 RING = 4
 CHIPS = RING**3
+STRIDE = 29
 HEAD = 64
 TILE_ROWS, LANES = 16, 128
 UNITS = 16
@@ -41,7 +42,8 @@
         return (self.at["z"] * RING + self.at["y"]) * RING + self.at["x"]
 
     def others(self):
-        for n in range(1, CHIPS):
+        for i in range(1, CHIPS):
+            n = i * STRIDE % CHIPS
             z, y, x = n // 16, n // 4 % 4, n % 4
             at = {"z": self.ring["z"][z], "y": self.ring["y"][y], "x": self.ring["x"][x]}
             yield self.device(at, self.core), (at["z"] * RING + at["y"]) * RING + at["x"]
@@ -63,6 +65,7 @@
 
 LINE, NEAR, FAR, PLANE, FAR_PLANE = (0, 16), (3, 32), (7, 16), (11, 32), (27, 64)
 RECV_COUNT = 31
+DIRECT = (2, 3)
 
 
 class Colour:
@@ -109,9 +112,13 @@
         own = self.piece(0, 0, 0)
         for slot, step in enumerate(STEPS):
             self.copy(own, 0, LINE, slot, step, self.own).start()
-        self.along_b(own, 0, self.own)
-        self.along_c(own, 0, 0, self.own)
-        self.give(own, self.own)
+
+    def open_b(self):
+        self.along_b(self.piece(0, 0, 0), 0, self.own)
+
+    def open_c(self):
+        self.along_c(self.piece(0, 0, 0), 0, 0, self.own)
+        self.give(self.piece(0, 0, 0), self.own)
 
     def line(self, t):
         ref = self.piece(0, 0, t)
@@ -133,12 +140,15 @@
 
     def far(self, t):
         self.along_c(self.piece(0, 2, t), 3, t)
+        if t in DIRECT:
+            self.copy(self.piece(0, 2, t), 2, FAR_PLANE, 3, 2).start()
         if t == 3:
             self.give(self.row(0, 2))
 
     def plane(self, n, t):
         plane, step = (3, 1) if t in (0, 3) else (1, 3)
-        self.copy(self.piece(plane, SOURCES[n], t), 2, FAR_PLANE, n, step).start()
+        if n < 3 or t not in DIRECT:
+            self.copy(self.piece(plane, SOURCES[n], t), 2, FAR_PLANE, n, step).start()
         if t == 3:
             for plane in (3, 1):
                 self.give(self.row(plane, SOURCES[n]))
@@ -154,13 +164,15 @@
         remote(self.held, other, self.share.at[0], self.share.at[1], self.sibling).wait()
 
 
-GATHER = [("open",)]
+GATHER = [("open",), ("open_b",), ("open_c",)]
 GATHER += [("line", t) for t in range(1, RING)]
 GATHER += [("line_on", t) for t in range(1, RING)]
 for _t in range(RING):
-    GATHER += [("near", _t), ("near_on", _t), ("plane", 0, _t)]
+    GATHER += [("near", _t), ("near_on", _t)]
 for _t in range(RING):
-    GATHER += [("far", _t), ("plane", 1, _t), ("plane", 2, _t)]
+    GATHER += [("plane", 0, _t), ("far", _t)]
+for _t in range(RING):
+    GATHER += [("plane", 1, _t), ("plane", 2, _t)]
 GATHER += [("plane", 3, _t) for _t in range(RING)]
 GATHER += [("far_plane", _n) for _n in range(RING)]
 
@@ -395,7 +407,7 @@
     def tiles(n):
         return tok.at[0, pl.ds(0, n * 2)]
 
-    gather(colours, tiles, {("open",): new_blocks, ("plane", 2, 3): [share_w]})
+    gather(colours, tiles, {("open_c",): new_blocks, ("plane", 2, 3): [share_w]})
     remote(w_mine, w_theirs, w_sems.at[2], w_sems.at[3], place.sibling()).wait()
 
     for n in range(RING):
@@ -408,22 +420,21 @@
         a, b, c = (by_core(core, at[p], at[q]) for p, q in zip(order_of(k, 0), order_of(k, 1)))
         return heads[k][c, b, a, u - COLOURS[k][0]]
 
-    def group_step(g, carry):
-        rows = [
-            jnp.concatenate([tile(g // 2, g % 2 * 2 + y, x, j * 2 + i) for j in range(8)], axis=1)
-            for x in range(RING)
-            for y in range(2)
-            for i in range(2)
-        ]
-        rhs = w_all[pl.ds(g * 8, 8)].reshape(8 * LANES, LANES)
-        parts = [
-            jnp.dot(jnp.concatenate(rows[n : n + 8], axis=0), rhs, preferred_element_type=jnp.float32) for n in (0, 8)
-        ]
-        for n, part in enumerate(parts):
-            total[n * 128 : (n + 1) * 128] += part
+    def group_step(n, carry):
+        parts = []
+        for g in (n, n + 4):
+            rows = [
+                jnp.concatenate([tile(g // 2, g % 2 * 2 + y, x, j * 2 + i) for j in range(8)], axis=1)
+                for x in range(RING)
+                for y in range(2)
+                for i in range(2)
+            ]
+            rhs = w_all[pl.ds(g * 8, 8)].reshape(8 * LANES, LANES)
+            parts.append(jnp.dot(jnp.concatenate(rows, axis=0), rhs, preferred_element_type=jnp.float32))
+        total[...] += parts[0] + parts[1]
         return carry
 
-    lax.fori_loop(0, 8, group_step, 0)
+    lax.fori_loop(0, 4, group_step, 0)
 
     out_colours = [
         Colour(place, outs[k].at[core], k, own_out.at[first:last], recv_out, send_out.at[k], share.at[k])

time: 77.2 us -> 71 us (0.920)
  Pallas kernels: 76.4 us -> 70.2 us
    pallas_call x1, Pallas kernels: 72.8 us -> 66.6 us  [whole_step(): pl.pallas_call(step_kernel, out_shape=[pltpu.VMEM((2, *shape), jnp.bfloat...]
where the time goes in v4:
time: 71 us; the launch traced here: 70.8 us
  Pallas kernels  70.2 us (99%)
    pallas_call x1, Pallas kernels, whole_step(): pl.pallas_call(step_kernel, out_shape=[pltpu.VMEM((2, *shape), jnp.bfloat...  66.6 us
    pallas_call x1, Pallas kernels, lay_out(): pl.pallas_call(lay_out_kernel, out_shape=[jax.ShapeDtypeStruct((512, CHIP...  3.61 us

profile of v4, /device:TPU:1, one launch (start us, length us, event | category | flops | bytes accessed | tf_op | source)
XLA Modules:
  0.0 70.8 jit_solution(17926614089662444168)
XLA Ops:
  0.6 66.6 %whole_step.1 = (bf16[2,4,4,4,5,16,128]{6,5,4,3,2,1,0:T(8,128)(2,1)S(1)}, bf16[2,4,4,4,5,16,128]{6,5,4,3,2,1,0:T(8,128)(2,1)S(1)}, bf16[2,4,4,4,6,16,128]{6,5,4,...) custom-call(bf16[512,8192]{1,0:T(8,128)(2,1)} %tokens.1, ...), custom_call_target="tpu_custom_call" | custom-call | tf_op jit(solution)/shard_map/whole_step/pallas_call | solution.py:456
  67.2 3.6 %lay_out.1 = (bf16[512,8192]{1,0:T(8,128)(2,1)}, bf16[64,8,64]{2,1,0:T(8,128)(2,1)}, bf16[64,8,64]{2,1,0:T(8,128)(2,1)}) custom-call(bf16[2,4,4,4,5,16,128]{6,5,4,3,2,1,0:T(8,128)(2,1)S(1)} %get-tuple-element.9.refs_0_, bf16[2,4,4,4,5,16,128]{6,5,4,3,2,1,0:T(8,128)(2,1)S(1)} %get-tuple-element.10.refs_1_, ...), custom_call_target="tpu_custom_call" | custom-call | tf_op jit(solution)/shard_map/lay_out/pallas_call | solution.py:535
